TPU v7x, 256 devices: a whole 4x4x8 slice. The times are simulated.
256 devices in a mesh: dp: 64 (over z, y, core), cp: 4 (over x).
Axes of the slice: x: 4, y: 4, z: 8, core: 2. Of those that a mesh axis runs over, the one named last changes fastest.
Arguments:
- hidden: bfloat16 [64, 2048, 2048], P('dp', 'cp')
- positions: int32 [2048], P('cp')
- w_q: bfloat16 [2048, 2048], replicated
- w_k: bfloat16 [2048, 2048], replicated
- w_v: bfloat16 [2048, 2048], replicated
- w_o: bfloat16 [2048, 2048], replicated
Outputs:
- output 1: bfloat16 [64, 2048, 2048], P('dp', 'cp')
- output 2: float32 [16], replicated
- output 3: bfloat16 [2048, 2048], replicated
- output 4: bfloat16 [2048, 2048], replicated
All inputs are finite; a program needn't handle non-finite values.
Results may differ from a plain program's by a relative error of at most 0.00783462.
Values are sent between devices in bfloat16 or wider.
A program may use at most 768 MiB of HBM per device.

v0:
```python
import jax
import jax.numpy as jnp
from jax import lax
from jax.sharding import PartitionSpec as P

HEAD_DIM = 128
TAU_CLIP = 100.0
ROPE_THETA = 50000.0


def rope_tables(pos_ids):
    half_dim = HEAD_DIM // 2
    inv_freq = jnp.float32(ROPE_THETA) ** (-jnp.arange(half_dim, dtype=jnp.float32) * (2.0 / HEAD_DIM))
    angle = pos_ids.astype(jnp.float32)[:, None] * inv_freq[None, :]
    return jnp.cos(angle)[None, :, None, :], jnp.sin(angle)[None, :, None, :]


def rope_rotate(tensor, cos_t, sin_t):
    half_dim = HEAD_DIM // 2
    lead_half = tensor[..., :half_dim]
    tail_half = tensor[..., half_dim:]
    return jnp.concatenate([lead_half * cos_t - tail_half * sin_t, tail_half * cos_t + lead_half * sin_t], axis=-1)


def project_heads(hidden, pos_ids, w_q, w_k, w_v):
    batch_n, seq_n, _ = hidden.shape
    head_shape = (batch_n, seq_n, w_q.shape[1] // HEAD_DIM, HEAD_DIM)
    cos_t, sin_t = rope_tables(pos_ids)
    q_heads = rope_rotate(jnp.dot(hidden, w_q, preferred_element_type=jnp.float32).reshape(head_shape), cos_t, sin_t).astype(jnp.bfloat16)
    k_heads = rope_rotate(jnp.dot(hidden, w_k, preferred_element_type=jnp.float32).reshape(head_shape), cos_t, sin_t).astype(jnp.bfloat16)
    v_heads = jnp.dot(hidden, w_v, preferred_element_type=jnp.float32).astype(jnp.bfloat16).reshape(head_shape)
    return q_heads, k_heads, v_heads


def empty_state(batch_n, seq_n, n_heads):
    row_shape = (batch_n, n_heads, seq_n)
    return (jnp.full(row_shape, -jnp.inf, jnp.float32), jnp.zeros(row_shape, jnp.float32),
            jnp.zeros((batch_n, seq_n, n_heads, HEAD_DIM), jnp.float32), jnp.full((n_heads,), -jnp.inf, jnp.float32))


def attend_block(q_heads, k_blk, v_blk, state, allowed):
    run_max, run_sum, out_acc, head_max = state
    scores = jnp.einsum("bqhd,bkhd->bhqk", q_heads, k_blk, preferred_element_type=jnp.float32) * (HEAD_DIM ** -0.5)
    if allowed is not None:
        scores = jnp.where(allowed, scores, -jnp.inf)
    head_max = jnp.maximum(head_max, jnp.max(scores, axis=(0, 2, 3)))
    new_max = jnp.maximum(run_max, jnp.max(scores, axis=-1))
    rescale = jnp.exp(run_max - new_max)
    prob_w = jnp.exp(scores - new_max[..., None])
    new_sum = run_sum * rescale + jnp.sum(prob_w, axis=-1)
    part_pv = jnp.einsum("bhqk,bkhd->bqhd", prob_w.astype(jnp.bfloat16), v_blk, preferred_element_type=jnp.float32)
    new_acc = out_acc * jnp.transpose(rescale, (0, 2, 1))[..., None] + part_pv
    return new_max, new_sum, new_acc, head_max


def finish_attn(state, w_o):
    run_max, run_sum, out_acc, head_max = state
    batch_n, seq_n, n_heads, _ = out_acc.shape
    attn_val = (out_acc / jnp.transpose(run_sum, (0, 2, 1))[..., None]).astype(jnp.bfloat16)
    attn_val = attn_val.reshape(batch_n, seq_n, n_heads * HEAD_DIM)
    return jnp.dot(attn_val, w_o, preferred_element_type=jnp.float32).astype(jnp.bfloat16), head_max


def clip_weights(head_max, w_q, w_k):
    factor = jnp.where(head_max > TAU_CLIP, jnp.sqrt(TAU_CLIP / head_max), 1.0)
    col_factor = jnp.repeat(factor, HEAD_DIM)[None, :]
    return (w_q.astype(jnp.float32) * col_factor).astype(jnp.bfloat16), (w_k.astype(jnp.float32) * col_factor).astype(jnp.bfloat16)


def solution(mesh):
    cp_size = mesh.shape["cp"]
    shift_pairs = [(src_rank, (src_rank + 1) % cp_size) for src_rank in range(cp_size)]

    def device_body(hidden, pos_ids, w_q, w_k, w_v, w_o):
        cp_rank = lax.axis_index("cp")
        q_heads, k_heads, v_heads = project_heads(hidden, pos_ids, w_q, w_k, w_v)
        batch_n, seq_n, n_heads, _ = q_heads.shape
        causal = lax.broadcasted_iota(jnp.int32, (seq_n, seq_n), 0) >= lax.broadcasted_iota(jnp.int32, (seq_n, seq_n), 1)
        state = attend_block(q_heads, k_heads, v_heads, empty_state(batch_n, seq_n, n_heads), causal)

        def step(step_idx, carried):
            k_blk, v_blk, attn_state = carried
            k_blk = lax.ppermute(k_blk, "cp", shift_pairs)
            v_blk = lax.ppermute(v_blk, "cp", shift_pairs)

            def use_block(state_in):
                return attend_block(q_heads, k_blk, v_blk, state_in, None)

            def skip_block(state_in):
                return state_in

            attn_state = lax.cond(step_idx <= cp_rank, use_block, skip_block, attn_state)
            return k_blk, v_blk, attn_state

        _, _, state = lax.fori_loop(1, cp_size, step, (k_heads, v_heads, state))
        attn_out, head_max = finish_attn(state, w_o)
        head_max = lax.pmax(head_max, ("dp", "cp"))
        w_q_new, w_k_new = clip_weights(head_max, w_q, w_k)
        return attn_out, head_max, w_q_new, w_k_new

    return jax.shard_map(
        device_body,
        mesh=mesh,
        in_specs=(P("dp", "cp", None), P("cp"), P(None, None), P(None, None), P(None, None), P(None, None)),
        out_specs=(P("dp", "cp", None), P(None), P(None, None), P(None, None)),
        check_vma=False,
    )
```

profile of v0, /device:TPU:6, one launch (start us, length us, event | category | flops | bytes accessed | tf_op | source)
XLA Modules:
  0.0 550.9 jit_solution(15797333661288473362)
XLA Ops:
  2.0 12.2 %copy.38 = bf16[2048,2048]{1,0:T(8,128)(2,1)} copy(bf16[2048,2048]{0,1:T(8,128)(2,1)} %bitcast.80) | data formatting | bytes 16777216 | tf_op jit(solution)/shard_map/dot_general | solution.py:29
  14.3 9.5 %convolution_bitcast_fusion = f32[1,512,16,128]{1,3,2,0:T(8,128)} fusion(bf16[16,128,2048]{2,1,0:T(8,128)(2,1)} %bitcast.84, bf16[1,512,2048]{2,1,0:T(8,128)(2,1)S(1)} %copy-done), kind=kOutput, calls=%fused_computation.36 | convolution fusion | flops 4294967296 | bytes 14680064 | tf_op jit(solution)/shard_map/dot_general | solution.py:29
  23.8 12.2 %copy.37 = bf16[2048,2048]{1,0:T(8,128)(2,1)} copy(bf16[2048,2048]{0,1:T(8,128)(2,1)} %bitcast.81) | data formatting | bytes 16777216 | tf_op jit(solution)/shard_map/dot_general | solution.py:30
  36.0 7.1 %convolution_bitcast_fusion.1 = f32[1,512,16,128]{1,3,2,0:T(8,128)S(1)} fusion(bf16[16,128,2048]{2,1,0:T(8,128)(2,1)} %bitcast.85, bf16[1,512,2048]{2,1,0:T(8,128)(2,1)S(1)} %copy-done), kind=kOutput, calls=%fused_computation.37 | convolution fusion | flops 4294967296 | bytes 14680064 | tf_op jit(solution)/shard_map/dot_general | solution.py:30
  51.6 5.9 %fusion.16 = (f32[16]{0:T(128)S(1)}, f32[16,512]{1,0:T(8,128)S(1)}) fusion(f32[16,512,512]{1,2,0:T(8,128)S(1)} %get-tuple-element.261, pred[512,512]{0,1:T(8,128)(4,1)S(1)} %iota_compare_fusion, f32[16,512]{1,0:T(8,128)S(1)} %get-tuple-element.260), kind=kLoop, calls=%fused_computation.24 | loop fusion | flops 20963312 | bytes 17104960 | tf_op jit(solution)/shard_map/reduce_max | solution.py:46
  57.5 9.1 %convolution_convert_fusion.1 = bf16[512,2048]{1,0:T(8,128)(2,1)} fusion(bf16[2048,2048]{1,0:T(8,128)(2,1)} %param.14, bf16[1,512,2048]{2,1,0:T(8,128)(2,1)S(1)} %copy-done), kind=kOutput, calls=%fused_computation.34 | convolution fusion | flops 4296015872 | bytes 12582912 | tf_op jit(solution)/shard_map/dot_general | solution.py:31
  69.4 12.3 %bitcast_add_fusion.2 = f32[1,512,16,128]{1,3,2,0:T(8,128)} fusion(bf16[512,16,128]{0,2,1:T(8,128)(2,1)S(1)} %bitcast.94, f32[16,512,512]{1,2,0:T(8,128)} %copy-done.2, f32[16,512]{1,0:T(8,128)S(1)} %get-tuple-element.260, pred[512,512]{0,1:T(8,128)(4,1)S(1)} %iota_compare_fusion, f32[512,16]{0,1:T(8,128)S(1)} %get-tuple-element.254), kind=kOutput, calls=%fused_computation.31 | convolution fusion | flops 1091567616 | bytes 23396352 | tf_op jit(solution)/shard_map/bhqk,bkhd->bqhd/dot_general | solution.py:51
  81.7 5.5 copy.30
  101.6 340.7 %while.23 = (s32[]{:T(128)}, bf16[1,512,16,128]{3,1,2,0:T(8,128)(2,1)S(1)}, bf16[1,512,16,128]{3,1,2,0:T(8,128)(2,1)}, f32[1,16,512]{2,1,0:T(8,128)S(1)}, f32[1,...) while((s32[]{:T(128)}, ...), condition=%wide.region_9.10_spmd, body=%wide.region_3.9_spmd.sunk | while | flops 2187354112 | bytes 90702400 | solution.py:95
  103.8 46.3 %collective-permute-done = bf16[1,512,16,128]{3,1,2,0:T(8,128)(2,1)} collective-permute-done((bf16[1,512,16,128]{3,1,2,0:T(8,128)(2,1)S(1)}, bf16[1,512,16,128]{3,1,2,0:T(8,128)(2,1)}, u32[]{:S(2)}, u32[]{:S(2)}) %collective-permute-start) | collective-permute-done | bytes 2097184 | tf_op jit(solution)/shard_map/while/body/eval_jaxpr/ppermute | solution.py:83
  150.1 43.8 %collective-permute-done.1 = bf16[1,512,16,128]{3,1,2,0:T(8,128)(2,1)} collective-permute-done((bf16[1,512,16,128]{3,1,2,0:T(8,128)(2,1)}, bf16[1,512,16,128]{3,1,2,0:T(8,128)(2,1)}, u32[]{:S(2)}, u32[]{:S(2)}) %collective-permute-start.1) | collective-permute-done | bytes 2097184 | tf_op jit(solution)/shard_map/while/body/eval_jaxpr/ppermute | solution.py:84
  193.9 17.3 %conditional.2 = ((f32[1,16,512]{2,1,0:T(8,128)S(1)}, f32[1,16,512]{2,1,0:T(8,128)S(1)}, f32[1,512,16,128]{3,1,2,0:T(8,128)}, f32[16]{0:T(128)S(1)})) conditional(s32[]{:T(128)} %convert_element_type.91, (f32[1,16,512]{2,1,0:T(8,128)S(1)}, f32[1,16,512]{2,1,0:T(8,128)S(1)}, f32[1,512,16,128]{3,1,2,0:T(8,128)}, f32[16]{0:T(128)S(1)}) %tuple.56, ...), branch_computations={%region_4.4_spmd, %region_5.8_spmd} | conditional | flops 2187354112 | bytes 65536296 | solution.py:92
  203.3 7.9 %bitcast_add_fusion = f32[1,512,16,128]{3,1,2,0:T(8,128)} fusion(f32[1,512,16,128]{3,1,2,0:T(8,128)} %get-tuple-element.177, f32[16,512,512]{1,2,0:T(8,128)S(1)} %get-tuple-element.247, f32[16,512]{1,0:T(8,128)S(1)} %bitcast.83, bf16[1,512,16,128]{3,1,2,0:T(8,128)(2,1)} %get-tuple-element.178, f32[512,16]{0,1:T(8,128)S(1)} %get-tuple-element.244), kind=kOutput, calls=%fused_computation.8 | convolution fusion | flops 1088421888 | bytes 27328512 | tf_op jit(solution)/shard_map/while/body/eval_jaxpr/cond/branch_1_fun/bhqk,bkhd->bqhd/dot_general | solution.py:51
  217.9 46.5 %collective-permute-done = bf16[1,512,16,128]{3,1,2,0:T(8,128)(2,1)} collective-permute-done((bf16[1,512,16,128]{3,1,2,0:T(8,128)(2,1)S(1)}, bf16[1,512,16,128]{3,1,2,0:T(8,128)(2,1)}, u32[]{:S(2)}, u32[]{:S(2)}) %collective-permute-start) | collective-permute-done | bytes 2097184 | tf_op jit(solution)/shard_map/while/body/eval_jaxpr/ppermute | solution.py:83
  264.4 43.1 %collective-permute-done.1 = bf16[1,512,16,128]{3,1,2,0:T(8,128)(2,1)} collective-permute-done((bf16[1,512,16,128]{3,1,2,0:T(8,128)(2,1)}, bf16[1,512,16,128]{3,1,2,0:T(8,128)(2,1)}, u32[]{:S(2)}, u32[]{:S(2)}) %collective-permute-start.1) | collective-permute-done | bytes 2097184 | tf_op jit(solution)/shard_map/while/body/eval_jaxpr/ppermute | solution.py:84
  307.5 17.3 %conditional.2 = ((f32[1,16,512]{2,1,0:T(8,128)S(1)}, f32[1,16,512]{2,1,0:T(8,128)S(1)}, f32[1,512,16,128]{3,1,2,0:T(8,128)}, f32[16]{0:T(128)S(1)})) conditional(s32[]{:T(128)} %convert_element_type.91, (f32[1,16,512]{2,1,0:T(8,128)S(1)}, f32[1,16,512]{2,1,0:T(8,128)S(1)}, f32[1,512,16,128]{3,1,2,0:T(8,128)}, f32[16]{0:T(128)S(1)}) %tuple.56, ...), branch_computations={%region_4.4_spmd, %region_5.8_spmd} | conditional | flops 2187354112 | bytes 65536296 | solution.py:92
  316.8 7.9 %bitcast_add_fusion = f32[1,512,16,128]{3,1,2,0:T(8,128)} fusion(f32[1,512,16,128]{3,1,2,0:T(8,128)} %get-tuple-element.177, f32[16,512,512]{1,2,0:T(8,128)S(1)} %get-tuple-element.247, f32[16,512]{1,0:T(8,128)S(1)} %bitcast.83, bf16[1,512,16,128]{3,1,2,0:T(8,128)(2,1)} %get-tuple-element.178, f32[512,16]{0,1:T(8,128)S(1)} %get-tuple-element.244), kind=kOutput, calls=%fused_computation.8 | convolution fusion | flops 1088421888 | bytes 27328512 | tf_op jit(solution)/shard_map/while/body/eval_jaxpr/cond/branch_1_fun/bhqk,bkhd->bqhd/dot_general | solution.py:51
  329.5 48.5 %collective-permute-done = bf16[1,512,16,128]{3,1,2,0:T(8,128)(2,1)} collective-permute-done((bf16[1,512,16,128]{3,1,2,0:T(8,128)(2,1)S(1)}, bf16[1,512,16,128]{3,1,2,0:T(8,128)(2,1)}, u32[]{:S(2)}, u32[]{:S(2)}) %collective-permute-start) | collective-permute-done | bytes 2097184 | tf_op jit(solution)/shard_map/while/body/eval_jaxpr/ppermute | solution.py:83
  378.0 42.3 %collective-permute-done.1 = bf16[1,512,16,128]{3,1,2,0:T(8,128)(2,1)} collective-permute-done((bf16[1,512,16,128]{3,1,2,0:T(8,128)(2,1)}, bf16[1,512,16,128]{3,1,2,0:T(8,128)(2,1)}, u32[]{:S(2)}, u32[]{:S(2)}) %collective-permute-start.1) | collective-permute-done | bytes 2097184 | tf_op jit(solution)/shard_map/while/body/eval_jaxpr/ppermute | solution.py:84
  420.3 17.3 %conditional.2 = ((f32[1,16,512]{2,1,0:T(8,128)S(1)}, f32[1,16,512]{2,1,0:T(8,128)S(1)}, f32[1,512,16,128]{3,1,2,0:T(8,128)}, f32[16]{0:T(128)S(1)})) conditional(s32[]{:T(128)} %convert_element_type.91, (f32[1,16,512]{2,1,0:T(8,128)S(1)}, f32[1,16,512]{2,1,0:T(8,128)S(1)}, f32[1,512,16,128]{3,1,2,0:T(8,128)}, f32[16]{0:T(128)S(1)}) %tuple.56, ...), branch_computations={%region_4.4_spmd, %region_5.8_spmd} | conditional | flops 2187354112 | bytes 65536296 | solution.py:92
  429.6 7.9 %bitcast_add_fusion = f32[1,512,16,128]{3,1,2,0:T(8,128)} fusion(f32[1,512,16,128]{3,1,2,0:T(8,128)} %get-tuple-element.177, f32[16,512,512]{1,2,0:T(8,128)S(1)} %get-tuple-element.247, f32[16,512]{1,0:T(8,128)S(1)} %bitcast.83, bf16[1,512,16,128]{3,1,2,0:T(8,128)(2,1)} %get-tuple-element.178, f32[512,16]{0,1:T(8,128)S(1)} %get-tuple-element.244), kind=kOutput, calls=%fused_computation.8 | convolution fusion | flops 1088421888 | bytes 27328512 | tf_op jit(solution)/shard_map/while/body/eval_jaxpr/cond/branch_1_fun/bhqk,bkhd->bqhd/dot_general | solution.py:51
  442.3 78.6 %pmax.7 = f32[16]{0:T(128)S(1)} all-reduce(f32[16]{0:T(128)S(1)} %get-tuple-element.203), channel_id=1, replica_groups=mesh['dp'=64,'cp'=4] {'dp','cp'}, use_global_device_ids=true, to_apply=%region_10.11 | all-reduce | flops 16 | bytes 128 | tf_op jit(solution)/shard_map/pmax | solution.py:97
  521.0 12.5 %multiply_convert_fusion = (bf16[2048,2048]{1,0:T(8,128)(2,1)}, bf16[2048,2048]{1,0:T(8,128)(2,1)}) fusion(bf16[2048,2048]{1,0:T(8,128)(2,1)} %param.13, f32[2048]{0:T(1024)S(1)} %broadcast_bitcast_fusion, bf16[2048,2048]{1,0:T(8,128)(2,1)} %param.12), kind=kLoop, calls=%fused_computation.18 | loop fusion | flops 25165824 | bytes 33562624 | tf_op jit(solution)/shard_map/convert_element_type | solution.py:67
  541.6 9.3 %fusion.24 = bf16[1,512,2048]{2,1,0:T(8,128)(2,1)} fusion(bf16[512,2048]{0,1:T(8,128)(2,1)S(1)} %bitcast.93, bf16[2048,2048]{1,0:T(8,128)(2,1)} %param.15), kind=kOutput, calls=%fused_computation.35 | convolution fusion | flops 4296015872 | bytes 12582912 | tf_op jit(solution)/shard_map/dot_general | solution.py:61
  (65 shorter events, 81.6 us)
Async XLA Ops:
  0.6 13.6 %copy-start = (bf16[1,512,2048]{2,1,0:T(8,128)(2,1)S(1)}, bf16[1,512,2048]{2,1,0:T(8,128)(2,1)}, u32[]{:S(2)}) copy-start(bf16[1,512,2048]{2,1,0:T(8,128)(2,1)} %param.10) | copy-start | bytes 6291460
  36.0 7.1 %copy-start.4 = (f32[1,512,16,128]{1,3,2,0:T(8,128)S(1)}, f32[1,512,16,128]{1,3,2,0:T(8,128)}, u32[]{:S(2)}) copy-start(f32[1,512,16,128]{1,3,2,0:T(8,128)} %convolution_bitcast_fusion) | copy-start | bytes 12582916
  51.6 5.9 %copy-start.2 = (f32[16,512,512]{1,2,0:T(8,128)}, f32[16,512,512]{1,2,0:T(8,128)S(1)}, u32[]{:S(2)}) copy-start(f32[16,512,512]{1,2,0:T(8,128)S(1)} %get-tuple-element.261) | copy-start | bytes 50331652
  81.7 5.5 copy-start.5
  81.7 5.5 copy-start.6
  91.2 8.0 %copy-start.3 = (bf16[512,2048]{1,0:T(8,128)(2,1)S(1)}, bf16[512,2048]{1,0:T(8,128)(2,1)}, u32[]{:S(2)}) copy-start(bf16[512,2048]{1,0:T(8,128)(2,1)} %convolution_convert_fusion.1) | copy-start | bytes 6291460
  99.7 1.9 copy-start.7
  101.6 48.5 %collective-permute-start = (bf16[1,512,16,128]{3,1,2,0:T(8,128)(2,1)S(1)}, bf16[1,512,16,128]{3,1,2,0:T(8,128)(2,1)}, u32[]{:S(2)}, u32[]{:S(2)}) collective-permute-start(bf16[1,512,16,128]{3,1,2,0:T(8,128)(2,1)S(1)} %get-tuple-element.346), channel_id=1, source_target_pairs={{0,1},{1,2},{2,3},{3,0},{4,5},{5,6},{6,7},{7,4},{8,9},{9,10},{10,1... | collective-permute-start | bytes 6291464 | tf_op jit(solution)/shard_map/while/body/eval_jaxpr/ppermute | solution.py:83
  103.8 90.2 %collective-permute-start.1 = (bf16[1,512,16,128]{3,1,2,0:T(8,128)(2,1)}, bf16[1,512,16,128]{3,1,2,0:T(8,128)(2,1)}, u32[]{:S(2)}, u32[]{:S(2)}) collective-permute-start(bf16[1,512,16,128]{3,1,2,0:T(8,128)(2,1)} %get-tuple-element.347), channel_id=1, source_target_pairs={{0,1},{1,2},{2,3},{3,0},{4,5},{5,6},{6,7},{7,4},{8,9},{9,10},{10,1... | collective-permute-start | bytes 6291464 | tf_op jit(solution)/shard_map/while/body/eval_jaxpr/ppermute | solution.py:84
  215.9 48.5 %collective-permute-start = (bf16[1,512,16,128]{3,1,2,0:T(8,128)(2,1)S(1)}, bf16[1,512,16,128]{3,1,2,0:T(8,128)(2,1)}, u32[]{:S(2)}, u32[]{:S(2)}) collective-permute-start(bf16[1,512,16,128]{3,1,2,0:T(8,128)(2,1)S(1)} %get-tuple-element.346), channel_id=1, source_target_pairs={{0,1},{1,2},{2,3},{3,0},{4,5},{5,6},{6,7},{7,4},{8,9},{9,10},{10,1... | collective-permute-start | bytes 6291464 | tf_op jit(solution)/shard_map/while/body/eval_jaxpr/ppermute | solution.py:83
  215.9 91.6 %collective-permute-start.1 = (bf16[1,512,16,128]{3,1,2,0:T(8,128)(2,1)}, bf16[1,512,16,128]{3,1,2,0:T(8,128)(2,1)}, u32[]{:S(2)}, u32[]{:S(2)}) collective-permute-start(bf16[1,512,16,128]{3,1,2,0:T(8,128)(2,1)} %get-tuple-element.347), channel_id=1, source_target_pairs={{0,1},{1,2},{2,3},{3,0},{4,5},{5,6},{6,7},{7,4},{8,9},{9,10},{10,1... | collective-permute-start | bytes 6291464 | tf_op jit(solution)/shard_map/while/body/eval_jaxpr/ppermute | solution.py:84
  329.5 48.5 %collective-permute-start = (bf16[1,512,16,128]{3,1,2,0:T(8,128)(2,1)S(1)}, bf16[1,512,16,128]{3,1,2,0:T(8,128)(2,1)}, u32[]{:S(2)}, u32[]{:S(2)}) collective-permute-start(bf16[1,512,16,128]{3,1,2,0:T(8,128)(2,1)S(1)} %get-tuple-element.346), channel_id=1, source_target_pairs={{0,1},{1,2},{2,3},{3,0},{4,5},{5,6},{6,7},{7,4},{8,9},{9,10},{10,1... | collective-permute-start | bytes 6291464 | tf_op jit(solution)/shard_map/while/body/eval_jaxpr/ppermute | solution.py:83
  329.5 90.8 %collective-permute-start.1 = (bf16[1,512,16,128]{3,1,2,0:T(8,128)(2,1)}, bf16[1,512,16,128]{3,1,2,0:T(8,128)(2,1)}, u32[]{:S(2)}, u32[]{:S(2)}) collective-permute-start(bf16[1,512,16,128]{3,1,2,0:T(8,128)(2,1)} %get-tuple-element.347), channel_id=1, source_target_pairs={{0,1},{1,2},{2,3},{3,0},{4,5},{5,6},{6,7},{7,4},{8,9},{9,10},{10,1... | collective-permute-start | bytes 6291464 | tf_op jit(solution)/shard_map/while/body/eval_jaxpr/ppermute | solution.py:84
  520.9 12.6 %copy-start.8 = (f32[16]{0:T(128)}, f32[16]{0:T(128)S(1)}, u32[]{:S(2)}) copy-start(f32[16]{0:T(128)S(1)} %pmax.7) | copy-start | bytes 196
  541.6 9.3 %copy-start.1 = (bf16[1,512,2048]{2,1,0:T(8,128)(2,1)S(1)}, bf16[1,512,2048]{2,1,0:T(8,128)(2,1)}, u32[]{:S(2)}) copy-start(bf16[1,512,2048]{2,1,0:T(8,128)(2,1)} %param.10) | copy-start | bytes 6291460
where the time goes:
time: 553 us; the launch traced here: 551 us
  waiting for transfers between devices  271 us (49%)
  matrix products  89.3 us (16%)
  blocking collectives  78.6 us (14%)
  local copies, waits for them, and re-layouts  62.8 us (11%)
  other arithmetic  44.6 us (8%)
    ppermute x3, waiting for transfers between devices, step(): k_blk = lax.ppermute(k_blk, 'cp', shift_pairs)  141 us
    ppermute x3, waiting for transfers between devices, step(): v_blk = lax.ppermute(v_blk, 'cp', shift_pairs)  129 us
    pmax x1, blocking collectives, device_body(): head_max = lax.pmax(head_max, ('dp', 'cp'))  78.6 us
    dot_general x4, matrix products, attend_block(): jnp.einsum('bhqk,bkhd->bqhd', prob_w.astype(jnp.bfloat16), v_blk, preferr...  36 us
    while x5, local copies, waits for them, and re-layouts, device_body(): _, _, state = lax.fori_loop(1, cp_size, step, (k_heads, v_heads, state))  20.7 us
    reduce_max x4, other arithmetic, attend_block(): head_max = jnp.maximum(head_max, jnp.max(scores, axis=(0, 2, 3)))  20 us
    dot_general x4, matrix products, attend_block(): jnp.einsum('bqhd,bkhd->bhqk', q_heads, k_blk, preferred_element_type=jnp....  18.4 us
    while x6, local copies, waits for them, and re-layouts  14.1 us
  transfers between devices with their start and end apart: 6, of which 6 were waited for; matrix products, arithmetic and copies ran while one was open for 0% of the time, Pallas kernels for 0%

commit v1 on v0

v1 whole, which is shorter than its diff:
```python
import functools

import jax
import jax.numpy as jnp
from jax import lax
from jax.experimental import pallas as pl
from jax.experimental.pallas import tpu as pltpu
from jax.sharding import PartitionSpec as P

HEAD_DIM = 128
TAU_CLIP = 100.0
ROPE_THETA = 50000.0
SCALE = HEAD_DIM ** -0.5
LOG2E = 1.4426950408889634
MESH = pl.DeviceIdType.MESH

PIECE = 512
HALF = 256
MODEL = 2048
COLS = 1024
HEADS = 8
OWN, FAR, NEAR, LAST = 0, 1, 2, 3
F32, BF16 = jnp.float32, jnp.bfloat16


def attend_kernel(hid, pos, freq, w_q, w_k, w_v, w_o, out, peak,
                  hbuf, wq, wk, wv, wo, qbuf, kbuf, vbuf, acc, run_max, run_sum, o_all, o_send, cos_t, sin_t, pos_all,
                  wsem, send, recv, psend, precv, osem):
    x = lax.axis_index("cp")
    d = lax.axis_index("dp")
    core = lax.rem(d, 2)
    home = core == x // 2
    away = core != x // 2
    partner = d + 1 - 2 * core
    pair = x + 1 - 2 * lax.rem(x, 2)
    far_x = 3 - x
    piece_of = (x, far_x, pair, 3 - pair)
    col0 = pl.multiple_of(core * COLS, COLS)

    def rows(kind, half):
        return pl.ds(pl.multiple_of(piece_of[kind] * PIECE + half * HALF, HALF), HALF)

    def remote(src, dst, s_sem, r_sem, dp, cp):
        return pltpu.make_async_remote_copy(src_ref=src, dst_ref=dst, send_sem=s_sem, recv_sem=r_sem,
                                            device_id={"dp": dp, "cp": cp}, device_id_type=MESH)

    w_copies = [pltpu.make_async_copy(src.at[:, pl.ds(col0, COLS)], dst, wsem.at[i])
                for i, (src, dst) in enumerate(((w_k, wk), (w_v, wv), (w_q, wq)))]
    w_copies.append(pltpu.make_async_copy(w_o, wo, wsem.at[3]))
    own_local = [pltpu.make_async_copy(hid.at[pl.ds(j * HALF, HALF), :], hbuf.at[rows(OWN, j), :], wsem.at[4 + j])
                 for j in range(2)]

    @pl.when(home)
    def _():
        for j in range(2):
            own_local[j].start()
    for copy in w_copies:
        copy.start()

    barrier = pltpu.get_barrier_semaphore()
    for k in range(1, 4):
        pl.semaphore_signal(barrier, inc=1, device_id={"dp": d, "cp": lax.rem(x + k, 4)}, device_id_type=MESH)
    pl.semaphore_signal(barrier, inc=1, device_id={"dp": partner, "cp": x}, device_id_type=MESH)
    pl.semaphore_wait(barrier, 4)

    def own_copy(j, to_pair):
        src = hid.at[pl.ds(j * HALF, HALF), :]
        dst = hbuf.at[rows(OWN, j), :]
        if to_pair:
            return remote(src, dst, send.at[j], recv.at[NEAR * 2 + j], d, pair)
        return remote(src, dst, send.at[2 + j], recv.at[OWN * 2 + j], partner, x)

    def away_copy(j):
        return remote(hid.at[pl.ds(j * HALF, HALF), :], hbuf.at[rows(OWN, j), :], send.at[12 + j], recv.at[FAR * 2 + j], d, far_x)

    def far_to_pair(j):
        return remote(hbuf.at[rows(FAR, j), :], hbuf.at[rows(FAR, j), :], send.at[4 + j], recv.at[LAST * 2 + j], d, pair)

    def to_partner(kind, j):
        return remote(hbuf.at[rows(kind, j), :], hbuf.at[rows(kind, j), :], send.at[4 + 2 * kind + j], recv.at[kind * 2 + j], partner, x)

    pos_copies = [remote(pos, pos_all.at[x], psend.at[k - 1], precv.at[k - 1], d, lax.rem(x + k, 4)) for k in range(1, 4)]
    for copy in pos_copies:
        copy.start()

    @pl.when(home)
    def _():
        @pl.when(x != 3)
        def _():
            for j in range(2):
                own_copy(j, True).start()
        for j in range(2):
            own_copy(j, False).start()

    @pl.when(away)
    def _():
        for j in range(2):
            away_copy(j).start()

    for copy in pos_copies:
        copy.wait_recv()

    def tables(kind):
        piece = piece_of[kind]
        row_i = lax.broadcasted_iota(jnp.int32, (128, 128), 0)
        col_i = lax.broadcasted_iota(jnp.int32, (128, 128), 1)
        sign = jnp.where(lax.broadcasted_iota(jnp.int32, (1, 128), 1) < 64, -1.0, 1.0)

        def block(b, carry):
            if kind == OWN:
                line = pos[pl.ds(b, 1), :]
            else:
                line = pos_all[pl.ds(piece, 1), pl.ds(b, 1), :].reshape(1, 128)
            line = jnp.broadcast_to(line.astype(F32), (128, 128))
            column = jnp.sum(jnp.where(row_i == col_i, line, 0.0), axis=1, keepdims=True)
            angle = column * freq[...]
            at = pl.ds(pl.multiple_of(piece * PIECE + b * 128, 128), 128)
            cos_t[at, :] = jnp.cos(angle)
            sin_t[at, :] = jnp.sin(angle) * sign
            return carry

        lax.fori_loop(0, 4, block, 0)

    def rotate(t, cos_v, sin_v):
        return (t * cos_v + pltpu.roll(t, 64, 1) * sin_v).astype(BF16)

    def project(kind, half, with_q):
        at = rows(kind, half)
        cos_v, sin_v = cos_t[at, :], sin_t[at, :]
        slot_rows = pl.ds(half * HALF, HALF)

        def block(n, carry):
            cols = pl.ds(pl.multiple_of(n * 256, 256), 256)
            h = hbuf[at, :]
            k2 = jnp.dot(h, wk[:, cols], preferred_element_type=F32)
            v2 = jnp.dot(h, wv[:, cols], preferred_element_type=F32)
            kbuf[at, cols] = jnp.concatenate([rotate(k2[:, :128], cos_v, sin_v), rotate(k2[:, 128:], cos_v, sin_v)], axis=1)
            vbuf[at, cols] = v2.astype(BF16)
            if with_q:
                q2 = jnp.dot(h, wq[:, cols], preferred_element_type=F32)
                qbuf[kind, slot_rows, cols] = jnp.concatenate(
                    [rotate(q2[:, :128], cos_v, sin_v), rotate(q2[:, 128:], cos_v, sin_v)], axis=1)
            return carry

        lax.fori_loop(0, 4, block, 0)

    def tile(slot, piece, diagonal):
        key0 = pl.multiple_of(piece * PIECE, PIECE)

        def head(h, carry):
            cols = pl.ds(pl.multiple_of(h * HEAD_DIM, HEAD_DIM), HEAD_DIM)
            for qb in range(2):
                n_keys = HALF * (qb + 1) if diagonal else PIECE
                at = pl.ds(qb * HALF, HALF)
                k = kbuf[pl.ds(key0, n_keys), cols]
                v = vbuf[pl.ds(key0, n_keys), cols]
                s = lax.dot_general(qbuf[slot, at, cols], k, (((1,), (1,)), ((), ())), preferred_element_type=F32)
                if diagonal:
                    q_i = lax.broadcasted_iota(jnp.int32, (HALF, n_keys), 0) + qb * HALF
                    s = jnp.where(q_i >= lax.broadcasted_iota(jnp.int32, (HALF, n_keys), 1), s, -jnp.inf)
                top = jnp.max(s, axis=1, keepdims=True)
                if diagonal:
                    new = jnp.broadcast_to(top, (HALF, 128))
                else:
                    old = run_max[slot, h, at, :]
                    new = jnp.maximum(old, top)
                p = jnp.exp2((s - jnp.concatenate([new] * (n_keys // 128), axis=1)) * (SCALE * LOG2E))
                total = jnp.broadcast_to(jnp.sum(p, axis=1, keepdims=True), (HALF, 128))
                part = jnp.dot(p.astype(BF16), v, preferred_element_type=F32)
                if not diagonal:
                    fade = jnp.exp2((old - new) * (SCALE * LOG2E))
                    total = total + run_sum[slot, h, at, :] * fade
                    part = part + acc[slot, at, cols] * fade
                run_max[slot, h, at, :] = new
                run_sum[slot, h, at, :] = total
                acc[slot, at, cols] = part
            return carry

        lax.fori_loop(0, HEADS, head, 0)

    def arrive(kind, j):
        @pl.when(home)
        def _():
            if kind == OWN:
                own_local[j].wait()
            else:
                away_copy(j).wait_recv() if kind == FAR else own_copy(j, True).wait_recv() if kind == NEAR else far_to_pair(j).wait_recv()
                if kind == FAR:
                    @pl.when(x != 0)
                    def _():
                        far_to_pair(j).start()
                to_partner(kind, j).start()

        @pl.when(away)
        def _():
            if kind == OWN:
                own_copy(j, False).wait_recv()
            else:
                to_partner(kind, j).wait_recv()

    w_copies[0].wait()
    tables(OWN)
    w_copies[1].wait()
    w_copies[2].wait()
    for j in range(2):
        arrive(OWN, j)
        project(OWN, j, True)
    tile(OWN, x, True)
    tables(FAR)
    tables(NEAR)
    tables(LAST)
    for j in range(2):
        arrive(FAR, j)
        project(FAR, j, True)

        @pl.when(x != 2)
        def _():
            arrive(NEAR, j)
            project(NEAR, j, False)
    tile(FAR, far_x, True)
    later = jnp.where(x < 2, FAR, OWN)
    tile(later, jnp.where(x < 2, x, far_x), False)

    @pl.when(x <= 1)
    def _():
        tile(FAR, pair, False)

    @pl.when((x == 1) | (x == 3))
    def _():
        tile(OWN, pair, False)

    @pl.when(x != 1)
    def _():
        for j in range(2):
            arrive(LAST, j)
            project(LAST, j, False)

    @pl.when((x == 0) | (x == 2))
    def _():
        tile(FAR, 3 - pair, False)

    @pl.when(x >= 2)
    def _():
        tile(OWN, 3 - pair, False)

    keep = jnp.where(home, OWN, FAR)
    give = 1 - keep

    def finish(slot, dst):
        def head(h, carry):
            cols = pl.ds(pl.multiple_of(h * HEAD_DIM, HEAD_DIM), HEAD_DIM)
            dst[:, cols] = (acc[slot, :, cols] / run_sum[slot, h, :, :]).astype(BF16)
            return carry
        lax.fori_loop(0, HEADS, head, 0)

    exchange = remote(o_send, o_all.at[core], osem.at[0], osem.at[1], partner, x)
    finish(give, o_send)
    exchange.start()
    finish(keep, o_all.at[core])

    peak[...] = jnp.full(peak.shape, -jnp.inf, F32)

    def head_top(h, carry):
        top = jnp.maximum(jnp.max(run_max[0, h, :, :], axis=0, keepdims=True), jnp.max(run_max[1, h, :, :], axis=0, keepdims=True))
        peak[pl.ds(core * HEADS + h, 1), :] = top * SCALE
        return carry

    lax.fori_loop(0, HEADS, head_top, 0)
    w_copies[3].wait()
    exchange.wait_recv()

    def out_block(n, carry):
        cols = pl.ds(pl.multiple_of(n * 256, 256), 256)
        out[:, cols] = (jnp.dot(o_all[0], wo[:COLS, cols], preferred_element_type=F32)
                        + jnp.dot(o_all[1], wo[COLS:, cols], preferred_element_type=F32)).astype(BF16)
        return carry

    lax.fori_loop(0, MODEL // 256, out_block, 0)

    exchange.wait_send()
    for copy in pos_copies:
        copy.wait_send()

    @pl.when(away)
    def _():
        for j in range(2):
            away_copy(j).wait_send()

    @pl.when(home)
    def _():
        for j in range(2):
            own_copy(j, False).wait_send()
            to_partner(FAR, j).wait_send()

        @pl.when(x != 3)
        def _():
            for j in range(2):
                own_copy(j, True).wait_send()

        @pl.when(x != 0)
        def _():
            for j in range(2):
                far_to_pair(j).wait_send()

        @pl.when(x != 2)
        def _():
            for j in range(2):
                to_partner(NEAR, j).wait_send()

        @pl.when(x != 1)
        def _():
            for j in range(2):
                to_partner(LAST, j).wait_send()


def attend(hid, pos, freq, w_q, w_k, w_v, w_o):
    any_spec = pl.BlockSpec(memory_space=pl.ANY)
    vmem = pl.BlockSpec(memory_space=pltpu.VMEM)
    return pl.pallas_call(
        attend_kernel,
        name="attend",
        out_shape=[jax.ShapeDtypeStruct((PIECE, MODEL), BF16), jax.ShapeDtypeStruct((2 * HEADS, 128), F32)],
        in_specs=[any_spec, vmem, vmem, any_spec, any_spec, any_spec, any_spec],
        out_specs=[vmem, vmem],
        scratch_shapes=[
            pltpu.VMEM((4 * PIECE, MODEL), BF16),
            pltpu.VMEM((MODEL, COLS), BF16), pltpu.VMEM((MODEL, COLS), BF16), pltpu.VMEM((MODEL, COLS), BF16),
            pltpu.VMEM((MODEL, MODEL), BF16),
            pltpu.VMEM((2, PIECE, COLS), BF16), pltpu.VMEM((4 * PIECE, COLS), BF16), pltpu.VMEM((4 * PIECE, COLS), BF16),
            pltpu.VMEM((2, PIECE, COLS), F32), pltpu.VMEM((2, HEADS, PIECE, 128), F32), pltpu.VMEM((2, HEADS, PIECE, 128), F32),
            pltpu.VMEM((2, PIECE, COLS), BF16), pltpu.VMEM((PIECE, COLS), BF16),
            pltpu.VMEM((4 * PIECE, 128), F32), pltpu.VMEM((4 * PIECE, 128), F32), pltpu.VMEM((4, 8, 128), jnp.int32),
            pltpu.SemaphoreType.DMA((6,)), pltpu.SemaphoreType.DMA((14,)), pltpu.SemaphoreType.DMA((8,)),
            pltpu.SemaphoreType.DMA((3,)), pltpu.SemaphoreType.DMA((3,)), pltpu.SemaphoreType.DMA((2,)),
        ],
        compiler_params=pltpu.CompilerParams(collective_id=0, has_side_effects=True, vmem_limit_bytes=67043328),
        cost_estimate=pl.CostEstimate(flops=31_000_000_000, bytes_accessed=26_000_000, transcendentals=11_000_000),
    )(hid, pos, freq, w_q, w_k, w_v, w_o)


def peak_kernel(sizes, peak, best, cur, slots, send, recv):
    n_z, n_y, n_x = sizes
    x = lax.axis_index("cp")
    d = lax.axis_index("dp")
    core, y, z = lax.rem(d, 2), lax.rem(d // 2, n_y), d // (2 * n_y)
    rounds = [
        [(d + 1 - 2 * core, x)],
        [(d, lax.rem(x + k, n_x)) for k in range(1, n_x)],
        [((z * n_y + lax.rem(y + k, n_y)) * 2 + core, x) for k in range(1, n_y)],
        [((lax.rem(z + k, n_z) * n_y + y) * 2 + core, x) for k in range(1, n_z)],
    ]
    barrier = pltpu.get_barrier_semaphore()
    total = 0
    for peers in rounds:
        for dp, cp in peers:
            pl.semaphore_signal(barrier, inc=1, device_id={"dp": dp, "cp": cp}, device_id_type=MESH)
            total += 1
    cur[0] = peak[...]
    pl.semaphore_wait(barrier, total)
    index = 0
    copies = []
    for r, peers in enumerate(rounds):
        batch = []
        for dp, cp in peers:
            batch.append((index, pltpu.make_async_remote_copy(
                src_ref=cur.at[r], dst_ref=slots.at[index], send_sem=send.at[index], recv_sem=recv.at[index],
                device_id={"dp": dp, "cp": cp}, device_id_type=MESH)))
            index += 1
        for _, copy in batch:
            copy.start()
        value = cur[r]
        for i, copy in batch:
            copy.wait_recv()
            value = jnp.maximum(value, slots[i])
        if r + 1 < len(rounds):
            cur[r + 1] = value
        else:
            best[...] = value
        copies += batch
    for _, copy in copies:
        copy.wait_send()


def global_peak(peak, sizes):
    n_copies = 1 + sum(n - 1 for n in sizes)
    vmem = pl.BlockSpec(memory_space=pltpu.VMEM)
    shape = peak.shape
    return pl.pallas_call(
        functools.partial(peak_kernel, sizes),
        name="global_peak",
        out_shape=jax.ShapeDtypeStruct(shape, F32),
        in_specs=[vmem], out_specs=vmem,
        scratch_shapes=[pltpu.VMEM((4,) + shape, F32), pltpu.VMEM((n_copies,) + shape, F32),
                        pltpu.SemaphoreType.DMA((n_copies,)), pltpu.SemaphoreType.DMA((n_copies,))],
        compiler_params=pltpu.CompilerParams(collective_id=1, has_side_effects=True),
        cost_estimate=pl.CostEstimate(flops=10_000_000, bytes_accessed=8192, transcendentals=0),
    )(peak)


def clip_weights(head_max, w_q, w_k):
    factor = jnp.where(head_max > TAU_CLIP, jnp.sqrt(TAU_CLIP / head_max), 1.0)
    col_factor = jnp.repeat(factor, HEAD_DIM)[None, :]
    return (w_q.astype(F32) * col_factor).astype(BF16), (w_k.astype(F32) * col_factor).astype(BF16)


def solution(mesh):
    cp_size, dp_size = mesh.shape["cp"], mesh.shape["dp"]
    sizes = (dp_size // 8, 4, cp_size)
    swap = []
    for quad in range(dp_size // 2):
        for x in range(cp_size):
            src_dp = 2 * quad + 1 - x // 2
            dst_x = cp_size - 1 - x
            dst_dp = 2 * quad + 1 - dst_x // 2
            swap.append((src_dp * cp_size + x, dst_dp * cp_size + dst_x))

    def device_body(hidden, pos_ids, w_q, w_k, w_v, w_o):
        half_dim = HEAD_DIM // 2
        inv_freq = jnp.float32(ROPE_THETA) ** (-jnp.arange(half_dim, dtype=F32) * (2.0 / HEAD_DIM))
        freq = jnp.concatenate([inv_freq, inv_freq])[None, :]
        pos = jnp.pad(pos_ids.reshape(4, 128), ((0, 4), (0, 0)))
        out, peak = attend(hidden[0], pos, freq, w_q, w_k, w_v, w_o)
        swapped = lax.ppermute(out, ("dp", "cp"), swap)
        head_max = global_peak(peak, sizes)[:, 0]
        w_q_new, w_k_new = clip_weights(head_max, w_q, w_k)
        home = lax.rem(lax.axis_index("dp"), 2) == lax.axis_index("cp") // 2
        return jnp.where(home, out, swapped)[None], head_max, w_q_new, w_k_new

    return jax.shard_map(
        device_body,
        mesh=mesh,
        in_specs=(P("dp", "cp", None), P("cp"), P(None, None), P(None, None), P(None, None), P(None, None)),
        out_specs=(P("dp", "cp", None), P(None), P(None, None), P(None, None)),
        check_vma=False,
    )
```

time: 553 us -> 146 us (0.26)
  the two profiles are of different devices: /device:TPU:6 before, /device:TPU:8 now
where the time goes in v1:
time: 146 us
  Pallas kernels  128 us (88%)
  other arithmetic  14.8 us (10%)
  local copies, waits for them, and re-layouts  2.17 us (1%)
    pallas_call x1, Pallas kernels, attend(): pl.pallas_call(attend_kernel, name='attend', out_shape=[jax.ShapeDtypeStr...  86.9 us
    pallas_call x1, Pallas kernels, global_peak(): pl.pallas_call(functools.partial(peak_kernel, sizes), name='global_peak',...  40.7 us
    convert_element_type x1, other arithmetic, clip_weights(): (w_k.astype(F32) * col_factor).astype(BF16)  12.6 us
  transfers between devices with their start and end apart: 1, of which 0 were waited for; matrix products, arithmetic and copies ran while one was open for 9% of the time, Pallas kernels for 28%

profile of v1, /device:TPU:8, one launch (start us, length us, event | category | flops | bytes accessed | tf_op | source)
XLA Modules:
  0.0 146.1 jit_solution(10741235889815354282)
XLA Ops:
  0.6 0.6 maximum_bitcast_fusion.freq
  1.2 1.3 pad.4.pos
  2.5 86.9 %attend.1 = (bf16[512,2048]{1,0:T(8,128)(2,1)}, f32[16,128]{1,0:T(8,128)}) custom-call(bf16[512,2048]{1,0:T(8,128)(2,1)} %bitcast.9, s32[8,128]{1,0:T(8,128)} %pad.4.pos, f32[1,128]{1,0:T(1,128)} %maximum_bitcast_fusion.freq, bf16[2048,2048]{1,0:T(8,128)(2,1)} %w_q.1, bf16[2048,2048]{1,0:T(8,128)(2,1)} %w_k.1, bf16[2048,2048]{1,0:T(8,128)(2,1)} %w_v.1, ...), custom_call_target="tpu_custom_call" | custom-call | flops 31000000512 | bytes 26000000 | tf_op jit(solution)/shard_map/attend/pallas_call | solution.py:319
  89.4 0.8 collective-permute-start
  90.2 40.7 %global_peak.1 = f32[16,128]{1,0:T(8,128)} custom-call(f32[16,128]{1,0:T(8,128)} %get-tuple-element.7.peak), custom_call_target="tpu_custom_call" | custom-call | flops 10000000 | bytes 8192 | tf_op jit(solution)/shard_map/global_peak/pallas_call | solution.py:388
  130.9 0.8 slice_reduce_fusion
  131.7 0.0 copy-start.1
  131.8 0.1 broadcast_bitcast_fusion
  131.9 0.0 copy-start
  131.9 12.6 %multiply_convert_fusion = (bf16[2048,2048]{1,0:T(8,128)(2,1)}, bf16[2048,2048]{1,0:T(8,128)(2,1)}) fusion(bf16[2048,2048]{1,0:T(8,128)(2,1)} %w_k.1, f32[2048]{0:T(1024)S(1)} %broadcast_bitcast_fusion, bf16[2048,2048]{1,0:T(8,128)(2,1)} %w_q.1), kind=kLoop, calls=%fused_computation | loop fusion | flops 25165824 | bytes 33562624 | tf_op jit(solution)/shard_map/convert_element_type | solution.py:403
  144.5 0.0 copy-done.1
  144.5 0.0 collective-permute-done
  144.5 0.0 copy-done
  144.5 1.6 %select_bitcast_fusion = bf16[1,512,2048]{2,1,0:T(8,128)(2,1)} fusion(bf16[512,2048]{1,0:T(8,128)(2,1)S(1)} %copy-done, bf16[512,2048]{1,0:T(8,128)(2,1)S(1)} %collective-permute-done, pred[]{:T(512)S(6)} %eq.3), kind=kLoop, calls=%fused_computation.2 | loop fusion | flops 1048576 | bytes 6291457 | tf_op jit(solution)/shard_map/broadcast_in_dim | solution.py:427
  (2 shorter events, 0.0 us)
Async XLA Ops:
  89.4 55.1 %collective-permute-start = (bf16[512,2048]{1,0:T(8,128)(2,1)}, bf16[512,2048]{1,0:T(8,128)(2,1)S(1)}, u32[]{:S(2)}, u32[]{:S(2)}) collective-permute-start(bf16[512,2048]{1,0:T(8,128)(2,1)} %get-tuple-element.6), channel_id=1, source_target_pairs={{4,3},{5,2},{2,5},{3,4},{12,11},{13,10},{10,13},{11,12},{20,19},{2... | collective-permute-start | bytes 6291464 | tf_op jit(solution)/shard_map/ppermute | solution.py:423
  131.7 12.7 %copy-start.1 = (f32[16]{0:T(128)}, f32[16]{0:T(128)S(1)}, u32[]{:S(2)}) copy-start(f32[16]{0:T(128)S(1)} %slice_reduce_fusion) | copy-start | bytes 196
  131.9 12.6 %copy-start = (bf16[512,2048]{1,0:T(8,128)(2,1)S(1)}, bf16[512,2048]{1,0:T(8,128)(2,1)}, u32[]{:S(2)}) copy-start(bf16[512,2048]{1,0:T(8,128)(2,1)} %get-tuple-element.6) | copy-start | bytes 6291460

commit v2 on v1

v2 whole, which is shorter than its diff:
```python
import functools

import jax
import jax.numpy as jnp
import numpy as np
from jax import lax
from jax.experimental import pallas as pl
from jax.experimental.pallas import tpu as pltpu
from jax.sharding import PartitionSpec as P

HEAD_DIM = 128
TAU_CLIP = 100.0
ROPE_THETA = 50000.0
SCALE = HEAD_DIM ** -0.5
LOG2E = 1.4426950408889634
MESH = pl.DeviceIdType.MESH

PIECE = 512
HALF = 256
MODEL = 2048
COLS = 1024
HEADS = 8
OWN, FAR, NEAR, LAST = 0, 1, 2, 3
TABLE_OF = (0, 0, 1, 0)
F32, BF16 = jnp.float32, jnp.bfloat16


def attend_kernel(hid, pos, freq, w_q, w_k, w_v, w_o, out, peak,
                  hbuf, wq, wk, wv, wo, qbuf, kbuf, vbuf, acc, run_max, run_sum, o_all, cos_t, sin_t, pos_all,
                  bias, top_all, wsem, send, recv, psend, precv, osem, tsend, trecv):
    x = lax.axis_index("cp")
    d = lax.axis_index("dp")
    core = lax.rem(d, 2)
    home = core == x // 2
    away = core != x // 2
    partner = d + 1 - 2 * core
    pair = x + 1 - 2 * lax.rem(x, 2)
    far_x = 3 - x
    piece_of = (x, far_x, pair, 3 - pair)
    col0 = pl.multiple_of(core * COLS, COLS)

    def rows(kind, half):
        return pl.ds(pl.multiple_of(piece_of[kind] * PIECE + half * HALF, HALF), HALF)

    def remote(src, dst, s_sem, r_sem, dp, cp):
        return pltpu.make_async_remote_copy(src_ref=src, dst_ref=dst, send_sem=s_sem, recv_sem=r_sem,
                                            device_id={"dp": dp, "cp": cp}, device_id_type=MESH)

    w_copies = [pltpu.make_async_copy(src.at[:, pl.ds(col0, COLS)], dst, wsem.at[i])
                for i, (src, dst) in enumerate(((w_k, wk), (w_v, wv), (w_q, wq)))]
    w_copies.append(pltpu.make_async_copy(w_o.at[:, pl.ds(COLS, COLS)], wo, wsem.at[3]))
    wo_low = pltpu.make_async_copy(w_o.at[:, pl.ds(0, COLS)], wq, wsem.at[6])

    def half_rows(j):
        return pl.ds(pl.multiple_of(j * HALF, HALF), HALF)

    def own_local(j):
        return pltpu.make_async_copy(hid.at[half_rows(j), :], hbuf.at[rows(OWN, j), :], wsem.at[4 + j])

    @pl.when(home)
    def _():
        for j in range(2):
            own_local(j).start()
    for copy in w_copies:
        copy.start()

    barrier = pltpu.get_barrier_semaphore()
    for k in range(1, 4):
        pl.semaphore_signal(barrier, inc=1, device_id={"dp": d, "cp": lax.rem(x + k, 4)}, device_id_type=MESH)
    pl.semaphore_signal(barrier, inc=1, device_id={"dp": partner, "cp": x}, device_id_type=MESH)
    pl.semaphore_wait(barrier, 4)

    def own_copy(j, to_pair):
        src = hid.at[half_rows(j), :]
        dst = hbuf.at[rows(OWN, j), :]
        if to_pair:
            return remote(src, dst, send.at[j], recv.at[NEAR * 2 + j], d, pair)
        return remote(src, dst, send.at[2 + j], recv.at[OWN * 2 + j], partner, x)

    def away_copy(j):
        return remote(hid.at[half_rows(j), :], hbuf.at[rows(OWN, j), :], send.at[12 + j], recv.at[FAR * 2 + j], d, far_x)

    def far_to_pair(j):
        return remote(hbuf.at[rows(FAR, j), :], hbuf.at[rows(FAR, j), :], send.at[4 + j], recv.at[LAST * 2 + j], d, pair)

    def to_partner(kind, j):
        return remote(hbuf.at[rows(kind, j), :], hbuf.at[rows(kind, j), :], send.at[4 + 2 * kind + j], recv.at[kind * 2 + j], partner, x)

    pos_copies = [remote(pos, pos_all.at[x], psend.at[k - 1], precv.at[k - 1], d, lax.rem(x + k, 4)) for k in range(1, 4)]
    for copy in pos_copies:
        copy.start()

    @pl.when(home)
    def _():
        @pl.when(x != 3)
        def _():
            for j in range(2):
                own_copy(j, True).start()
        for j in range(2):
            own_copy(j, False).start()

    @pl.when(away)
    def _():
        for j in range(2):
            away_copy(j).start()

    def tables(kind):
        piece = piece_of[kind]
        row_i = lax.broadcasted_iota(jnp.int32, (64, 128), 0)
        col_i = lax.broadcasted_iota(jnp.int32, (64, 128), 1)
        low = col_i < 64

        def block(b, carry):
            if kind == OWN:
                line = pos[pl.ds(b, 1), :]
            else:
                line = pos_all[pl.ds(piece, 1), pl.ds(b, 1), :].reshape(1, 128)
            line = jnp.broadcast_to(line.astype(F32), (64, 128))
            first = jnp.sum(jnp.where(row_i == col_i, line, 0.0), axis=1, keepdims=True)
            second = jnp.sum(jnp.where(row_i + 64 == col_i, line, 0.0), axis=1, keepdims=True)
            angle = jnp.where(low, first, second) * freq[...]
            cos_a, sin_a = jnp.cos(angle), jnp.sin(angle)
            cos_r, sin_r = pltpu.roll(cos_a, 64, 1), pltpu.roll(sin_a, 64, 1)
            at = pl.multiple_of(TABLE_OF[kind] * PIECE + b * 128, 128)
            cos_t[pl.ds(at, 64), :] = jnp.where(low, cos_a, cos_r)
            cos_t[pl.ds(at + 64, 64), :] = jnp.where(low, cos_r, cos_a)
            sin_t[pl.ds(at, 64), :] = jnp.where(low, -sin_a, sin_r)
            sin_t[pl.ds(at + 64, 64), :] = jnp.where(low, -sin_r, sin_a)
            return carry

        lax.fori_loop(0, 4, block, 0)

    def rotate(t, cos_v, sin_v):
        parts = []
        for h in range(HEADS):
            u = t[:, h * HEAD_DIM:(h + 1) * HEAD_DIM]
            parts.append((u * cos_v + pltpu.roll(u, 64, 1) * sin_v).astype(BF16))
        return jnp.concatenate(parts, axis=1)

    def project(kind, half, with_q):
        at = rows(kind, half)
        table = pl.ds(pl.multiple_of(TABLE_OF[kind] * PIECE + half * HALF, HALF), HALF)
        cos_v, sin_v = cos_t[table, :], sin_t[table, :]
        h = hbuf[at, :]
        kbuf[at, :] = rotate(jnp.dot(h, wk[...], preferred_element_type=F32), cos_v, sin_v)
        vbuf[at, :] = jnp.dot(h, wv[...], preferred_element_type=F32).astype(BF16)
        if with_q:
            q_at = pl.ds(pl.multiple_of(half * HALF, HALF), HALF)
            qbuf[kind, q_at, :] = rotate(jnp.dot(h, wq[...], preferred_element_type=F32), cos_v, sin_v)

    def tile(slot, piece, diagonal):
        key0 = pl.multiple_of(piece * PIECE, PIECE)
        units = [(h, qb) for h in range(HEADS) for qb in range(2)]

        def scores(h, qb):
            n_keys = HALF * (qb + 1) if diagonal else PIECE
            cols = pl.ds(h * HEAD_DIM, HEAD_DIM)
            s = lax.dot_general(qbuf[slot, pl.ds(qb * HALF, HALF), cols], kbuf[pl.ds(key0, n_keys), cols],
                                (((1,), (1,)), ((), ())), preferred_element_type=F32)
            if diagonal:
                last = s[:, n_keys - HALF:] + bias[...]
                s = last if qb == 0 else jnp.concatenate([s[:, :n_keys - HALF], last], axis=1)
            return s

        results = []
        s = scores(*units[0])
        for i, (h, qb) in enumerate(units):
            s_next = scores(*units[i + 1]) if i + 1 < len(units) else None
            at = pl.ds(qb * HALF, HALF)
            n_keys = s.shape[1]
            top = jnp.max(s, axis=1, keepdims=True)
            old = None if diagonal else run_max[slot, h, at, :]
            new = jnp.broadcast_to(top, (HALF, 128)) if diagonal else jnp.maximum(old, top)
            p = jnp.exp2((s - jnp.concatenate([new] * (n_keys // 128), axis=1)) * (SCALE * LOG2E))
            total = p[:, :128]
            for g in range(1, n_keys // 128):
                total = total + p[:, g * 128:(g + 1) * 128]
            part = jnp.dot(p.astype(BF16), vbuf[pl.ds(key0, n_keys), pl.ds(h * HEAD_DIM, HEAD_DIM)],
                           preferred_element_type=F32)
            results.append((old, new, total, part))
            s = s_next
        for (h, qb), (old, new, total, part) in zip(units, results):
            at, cols = pl.ds(qb * HALF, HALF), pl.ds(h * HEAD_DIM, HEAD_DIM)
            if not diagonal:
                fade = jnp.exp2((old - new) * (SCALE * LOG2E))
                total = total + run_sum[slot, h, at, :] * fade
                part = part + acc[slot, at, cols] * fade
            run_max[slot, h, at, :] = new
            run_sum[slot, h, at, :] = total
            acc[slot, at, cols] = part

    def arrive(kind, j):
        @pl.when(home)
        def _():
            if kind == OWN:
                own_local(j).wait()
            else:
                away_copy(j).wait_recv() if kind == FAR else own_copy(j, True).wait_recv() if kind == NEAR else far_to_pair(j).wait_recv()
                if kind == FAR:
                    @pl.when(x != 0)
                    def _():
                        far_to_pair(j).start()
                to_partner(kind, j).start()

        @pl.when(away)
        def _():
            if kind == OWN:
                own_copy(j, False).wait_recv()
            else:
                to_partner(kind, j).wait_recv()

    bias[...] = jnp.where(lax.broadcasted_iota(jnp.int32, (HALF, HALF), 0) >= lax.broadcasted_iota(jnp.int32, (HALF, HALF), 1),
                          0.0, -jnp.inf)
    tables(OWN)
    for i in range(3):
        w_copies[i].wait()

    def own_half(j, carry):
        arrive(OWN, j)
        project(OWN, j, True)
        return carry

    lax.fori_loop(0, 2, own_half, 0)
    for copy in pos_copies:
        copy.wait_recv()
    tables(FAR)
    tables(NEAR)

    def far_half(j, carry):
        arrive(FAR, j)
        project(FAR, j, True)

        @pl.when(x != 2)
        def _():
            arrive(NEAR, j)
            project(NEAR, j, False)
        return carry

    lax.fori_loop(0, 2, far_half, 0)
    wo_low.start()
    tables(LAST)

    def diagonal_tile(slot, carry):
        tile(slot, jnp.where(slot == OWN, x, far_x), True)
        return carry

    lax.fori_loop(0, 2, diagonal_tile, 0)

    later = jnp.where(x < 2, FAR, OWN)

    def near_tile(i, carry):
        slot = jnp.where(i == 0, later, i - 1)
        piece = jnp.where(i == 0, jnp.minimum(x, far_x), pair)

        @pl.when((i == 0) | ((i == 1) & (lax.rem(x, 2) == 1)) | ((i == 2) & (x < 2)))
        def _():
            tile(slot, piece, False)
        return carry

    lax.fori_loop(0, 3, near_tile, 0)

    exchange = remote(qbuf.at[jnp.where(home, FAR, OWN)], o_all.at[core], osem.at[0], osem.at[1], partner, x)

    own_rows = pl.ds(pl.multiple_of(x * PIECE, PIECE), PIECE)

    def out_copy(part):
        cols = pl.ds(part * COLS, COLS)
        return pltpu.make_async_copy(hbuf.at[own_rows, cols], out.at[:, cols], wsem.at[7 + part])

    def section(slot):
        mine = (home & (slot == OWN)) | (away & (slot == FAR))

        def head(h, carry):
            cols = pl.ds(pl.multiple_of(h * HEAD_DIM, HEAD_DIM), HEAD_DIM)
            total = jnp.sum(run_sum[slot, h, :, :], axis=1, keepdims=True)
            value = (acc[slot, :, cols] / total).astype(BF16)

            @pl.when(mine)
            def _():
                o_all[core, :, cols] = value

            @pl.when(jnp.logical_not(mine))
            def _():
                qbuf[slot, :, cols] = value
            return carry

        lax.fori_loop(0, HEADS, head, 0)

        @pl.when(jnp.logical_not(mine))
        def _():
            exchange.start()

        @pl.when(mine)
        def _():
            exchange.wait_recv()

            for part, w in enumerate((wq, wo)):
                def out_block(n, carry):
                    cols = pl.ds(pl.multiple_of(n * 512, 512), 512)
                    value = (jnp.dot(o_all[0], w[:COLS, cols], preferred_element_type=F32)
                             + jnp.dot(o_all[1], w[COLS:, cols], preferred_element_type=F32))
                    hbuf[own_rows, pl.ds(pl.multiple_of(part * COLS + n * 512, 512), 512)] = value.astype(BF16)
                    return carry

                lax.fori_loop(0, COLS // 512, out_block, 0)
                out_copy(part).start()

    w_copies[3].wait()
    wo_low.wait()
    outer = (x == 0) | (x == 3)

    @pl.when(outer)
    def _():
        section(1 - later)

    @pl.when(x != 1)
    def _():
        def last_half(j, carry):
            arrive(LAST, j)
            project(LAST, j, False)
            return carry
        lax.fori_loop(0, 2, last_half, 0)

    def last_tile(slot, carry):
        @pl.when(((slot == OWN) & (x >= 2)) | ((slot == FAR) & (lax.rem(x, 2) == 0)))
        def _():
            tile(slot, 3 - pair, False)
        return carry

    lax.fori_loop(0, 2, last_tile, 0)

    top_all[0] = jnp.full((2 * HEADS, 128), -jnp.inf, F32)

    def head_top(h, carry):
        top = jnp.maximum(jnp.max(run_max[0, h, :, :], axis=0, keepdims=True), jnp.max(run_max[1, h, :, :], axis=0, keepdims=True))
        top_all[0, pl.ds(core * HEADS + h, 1), :] = top * SCALE
        return carry

    lax.fori_loop(0, HEADS, head_top, 0)
    top_copies = [remote(top_all.at[0], top_all.at[k], tsend.at[k - 1], trecv.at[k - 1], d, lax.rem(x + k, 4)) for k in range(1, 4)]
    for copy in top_copies:
        copy.start()

    def end_section(i, carry):
        section(jnp.where(i == 0, 1 - later, later))
        return carry

    lax.fori_loop(jnp.where(outer, 1, 0), 2, end_section, 0)

    best = top_all[0]
    for k, copy in enumerate(top_copies):
        copy.wait_recv()
        best = jnp.maximum(best, top_all[k + 1])
    peak[...] = best
    for copy in top_copies:
        copy.wait_send()

    for part in range(2):
        out_copy(part).wait()

    exchange.wait_send()
    for copy in pos_copies:
        copy.wait_send()

    @pl.when(away)
    def _():
        for j in range(2):
            away_copy(j).wait_send()

    @pl.when(home)
    def _():
        for j in range(2):
            own_copy(j, False).wait_send()
            to_partner(FAR, j).wait_send()

        @pl.when(x != 3)
        def _():
            for j in range(2):
                own_copy(j, True).wait_send()

        @pl.when(x != 0)
        def _():
            for j in range(2):
                far_to_pair(j).wait_send()

        @pl.when(x != 2)
        def _():
            for j in range(2):
                to_partner(NEAR, j).wait_send()

        @pl.when(x != 1)
        def _():
            for j in range(2):
                to_partner(LAST, j).wait_send()


def attend(hid, pos, freq, w_q, w_k, w_v, w_o):
    any_spec = pl.BlockSpec(memory_space=pl.ANY)
    vmem = pl.BlockSpec(memory_space=pltpu.VMEM)
    return pl.pallas_call(
        attend_kernel,
        name="attend",
        out_shape=[jax.ShapeDtypeStruct((PIECE, MODEL), BF16), jax.ShapeDtypeStruct((2 * HEADS, 128), F32)],
        in_specs=[any_spec, vmem, vmem, any_spec, any_spec, any_spec, any_spec],
        out_specs=[any_spec, vmem],
        scratch_shapes=[
            pltpu.VMEM((4 * PIECE, MODEL), BF16),
            pltpu.VMEM((MODEL, COLS), BF16), pltpu.VMEM((MODEL, COLS), BF16), pltpu.VMEM((MODEL, COLS), BF16),
            pltpu.VMEM((MODEL, COLS), BF16),
            pltpu.VMEM((2, PIECE, COLS), BF16), pltpu.VMEM((4 * PIECE, COLS), BF16), pltpu.VMEM((4 * PIECE, COLS), BF16),
            pltpu.VMEM((2, PIECE, COLS), F32), pltpu.VMEM((2, HEADS, PIECE, 128), F32), pltpu.VMEM((2, HEADS, PIECE, 128), F32),
            pltpu.VMEM((2, PIECE, COLS), BF16),
            pltpu.VMEM((2 * PIECE, 128), F32), pltpu.VMEM((2 * PIECE, 128), F32), pltpu.VMEM((4, 4, 128), jnp.int32),
            pltpu.VMEM((HALF, HALF), F32), pltpu.VMEM((4, 2 * HEADS, 128), F32),
            pltpu.SemaphoreType.DMA((9,)), pltpu.SemaphoreType.DMA((14,)), pltpu.SemaphoreType.DMA((8,)),
            pltpu.SemaphoreType.DMA((3,)), pltpu.SemaphoreType.DMA((3,)), pltpu.SemaphoreType.DMA((2,)),
            pltpu.SemaphoreType.DMA((3,)), pltpu.SemaphoreType.DMA((3,)),
        ],
        compiler_params=pltpu.CompilerParams(collective_id=0, has_side_effects=True, vmem_limit_bytes=67043328),
        cost_estimate=pl.CostEstimate(flops=31_000_000_000, bytes_accessed=26_000_000, transcendentals=11_000_000),
    )(hid, pos, freq, w_q, w_k, w_v, w_o)


def peak_kernel(sizes, peak, best, cur, slots, send, recv):
    n_z, n_y = sizes
    x = lax.axis_index("cp")
    d = lax.axis_index("dp")
    core, y, z = lax.rem(d, 2), lax.rem(d // 2, n_y), d // (2 * n_y)
    rounds = [
        [(d + 1 - 2 * core, x)],
        [((z * n_y + lax.rem(y + k, n_y)) * 2 + core, x) for k in range(1, n_y)],
        [((lax.rem(z + k, n_z) * n_y + y) * 2 + core, x) for k in range(1, n_z)],
    ]
    barrier = pltpu.get_barrier_semaphore()
    total = 0
    for peers in rounds:
        for dp, cp in peers:
            pl.semaphore_signal(barrier, inc=1, device_id={"dp": dp, "cp": cp}, device_id_type=MESH)
            total += 1
    cur[0] = peak[...]
    pl.semaphore_wait(barrier, total)
    index = 0
    copies = []
    for r, peers in enumerate(rounds):
        batch = []
        for dp, cp in peers:
            batch.append((index, pltpu.make_async_remote_copy(
                src_ref=cur.at[r], dst_ref=slots.at[index], send_sem=send.at[index], recv_sem=recv.at[index],
                device_id={"dp": dp, "cp": cp}, device_id_type=MESH)))
            index += 1
        for _, copy in batch:
            copy.start()
        value = cur[r]
        for i, copy in batch:
            copy.wait_recv()
            value = jnp.maximum(value, slots[i])
        if r + 1 < len(rounds):
            cur[r + 1] = value
        else:
            best[...] = value
        copies += batch
    for _, copy in copies:
        copy.wait_send()


def global_peak(peak, sizes):
    n_copies = 1 + sum(n - 1 for n in sizes)
    vmem = pl.BlockSpec(memory_space=pltpu.VMEM)
    shape = peak.shape
    return pl.pallas_call(
        functools.partial(peak_kernel, sizes),
        name="global_peak",
        out_shape=jax.ShapeDtypeStruct(shape, F32),
        in_specs=[vmem], out_specs=vmem,
        scratch_shapes=[pltpu.VMEM((3,) + shape, F32), pltpu.VMEM((n_copies,) + shape, F32),
                        pltpu.SemaphoreType.DMA((n_copies,)), pltpu.SemaphoreType.DMA((n_copies,))],
        compiler_params=pltpu.CompilerParams(collective_id=1, has_side_effects=True),
        cost_estimate=pl.CostEstimate(flops=10_000_000, bytes_accessed=8192, transcendentals=0),
    )(peak)


def clip_weights(head_max, w_q, w_k):
    factor = jnp.where(head_max > TAU_CLIP, jnp.sqrt(TAU_CLIP / head_max), 1.0)
    col_factor = jnp.repeat(factor, HEAD_DIM)[None, :]
    return (w_q.astype(F32) * col_factor).astype(BF16), (w_k.astype(F32) * col_factor).astype(BF16)


def solution(mesh):
    cp_size, dp_size = mesh.shape["cp"], mesh.shape["dp"]
    sizes = (dp_size // 8, 4)
    swap = []
    for quad in range(dp_size // 2):
        for x in range(cp_size):
            src_dp = 2 * quad + 1 - x // 2
            dst_x = cp_size - 1 - x
            dst_dp = 2 * quad + 1 - dst_x // 2
            swap.append((src_dp * cp_size + x, dst_dp * cp_size + dst_x))
            home = (2 * quad + x // 2) * cp_size + x
            swap.append((home, home))

    def device_body(hidden, pos_ids, w_q, w_k, w_v, w_o):
        inv_freq = ROPE_THETA ** (-np.arange(HEAD_DIM // 2) * (2.0 / HEAD_DIM))
        freq = jnp.asarray(np.concatenate([inv_freq, inv_freq])[None, :], F32)
        out, peak = attend(hidden[0], pos_ids.reshape(4, 128), freq, w_q, w_k, w_v, w_o)
        swapped = lax.ppermute(out, ("dp", "cp"), swap)
        head_max = global_peak(peak, sizes)[:, 0]
        w_q_new, w_k_new = clip_weights(head_max, w_q, w_k)
        return swapped[None], head_max, w_q_new, w_k_new

    return jax.shard_map(
        device_body,
        mesh=mesh,
        in_specs=(P("dp", "cp", None), P("cp"), P(None, None), P(None, None), P(None, None), P(None, None)),
        out_specs=(P("dp", "cp", None), P(None), P(None, None), P(None, None)),
        check_vma=False,
    )
```

time: 146 us -> 113 us (0.77)
  the two profiles are of different devices: /device:TPU:8 before, /device:TPU:6 now
where the time goes in v2:
time: 113 us
  Pallas kernels  87.6 us (78%)
  other arithmetic  12.5 us (11%)
  starting transfers between devices  10 us (9%)
  local copies, waits for them, and re-layouts  2.21 us (2%)
    pallas_call x1, Pallas kernels, attend(): pl.pallas_call(attend_kernel, name='attend', out_shape=[jax.ShapeDtypeStr...  70.7 us
    pallas_call x1, Pallas kernels, global_peak(): pl.pallas_call(functools.partial(peak_kernel, sizes), name='global_peak',...  16.9 us
    convert_element_type x1, other arithmetic, clip_weights(): (w_k.astype(F32) * col_factor).astype(BF16)  12.5 us
    ppermute x1, starting transfers between devices, device_body(): swapped = lax.ppermute(out, ('dp', 'cp'), swap)  10 us
  transfers between devices with their start and end apart: 1, of which 0 were waited for; matrix products, arithmetic and copies ran while one was open for 12% of the time, Pallas kernels for 15%

profile of v2, /device:TPU:6, one launch (start us, length us, event | category | flops | bytes accessed | tf_op | source)
XLA Modules:
  0.0 113.0 jit_solution(2605170772323937361)
XLA Ops:
  0.6 70.7 %attend.1 = (bf16[512,2048]{1,0:T(8,128)(2,1)}, f32[16,128]{1,0:T(8,128)}) custom-call(bf16[512,2048]{1,0:T(8,128)(2,1)} %bitcast.6, s32[4,128]{1,0:T(4,128)} %bitcast.7, f32[1,128]{1,0:T(1,128)} %constant.6.clone.freq, bf16[2048,2048]{1,0:T(8,128)(2,1)} %w_q.1, bf16[2048,2048]{1,0:T(8,128)(2,1)} %w_k.1, bf16[2048,2048]{1,0:T(8,128)(2,1)} %w_v.1, ...), custom_call_target="tpu_custom_call" | custom-call | flops 31000000512 | bytes 26000000 | tf_op jit(solution)/shard_map/attend/pallas_call | solution.py:400
  71.4 10.0 %collective-permute-start = (bf16[512,2048]{1,0:T(8,128)(2,1)}, bf16[512,2048]{1,0:T(8,128)(2,1)S(1)}, u32[]{:S(2)}, u32[]{:S(2)}) collective-permute-start(bf16[512,2048]{1,0:T(8,128)(2,1)} %get-tuple-element.6), channel_id=1, source_target_pairs={{4,3},{0,0},{5,2},{1,1},{2,5},{6,6},{3,4},{7,7},{12,11},{8,8},{13,... | collective-permute-start | bytes 6291464 | tf_op jit(solution)/shard_map/ppermute | solution.py:505
  81.4 16.9 %global_peak.1 = f32[16,128]{1,0:T(8,128)} custom-call(f32[16,128]{1,0:T(8,128)} %get-tuple-element.7.peak), custom_call_target="tpu_custom_call" | custom-call | flops 10000000 | bytes 8192 | tf_op jit(solution)/shard_map/global_peak/pallas_call | solution.py:470
  98.2 0.8 slice_reduce_fusion
  99.1 0.0 copy-start
  99.1 0.1 broadcast_bitcast_fusion
  99.2 12.5 %multiply_convert_fusion = (bf16[2048,2048]{1,0:T(8,128)(2,1)}, bf16[2048,2048]{1,0:T(8,128)(2,1)}) fusion(bf16[2048,2048]{1,0:T(8,128)(2,1)} %w_k.1, f32[2048]{0:T(1024)S(1)} %broadcast_bitcast_fusion, bf16[2048,2048]{1,0:T(8,128)(2,1)} %w_q.1), kind=kLoop, calls=%fused_computation | loop fusion | flops 25165824 | bytes 33562624 | tf_op jit(solution)/shard_map/convert_element_type | solution.py:485
  111.7 0.0 copy-done
  111.7 0.0 collective-permute-done
  111.7 1.3 %copy.12 = bf16[1,512,2048]{2,1,0:T(8,128)(2,1)} copy(bf16[1,512,2048]{2,1,0:T(8,128)(2,1)S(1)} %bitcast.5) | data formatting | bytes 4194304
  (1 shorter events, 0.0 us)
Async XLA Ops:
  71.4 40.3 %collective-permute-start = (bf16[512,2048]{1,0:T(8,128)(2,1)}, bf16[512,2048]{1,0:T(8,128)(2,1)S(1)}, u32[]{:S(2)}, u32[]{:S(2)}) collective-permute-start(bf16[512,2048]{1,0:T(8,128)(2,1)} %get-tuple-element.6), channel_id=1, source_target_pairs={{4,3},{0,0},{5,2},{1,1},{2,5},{6,6},{3,4},{7,7},{12,11},{8,8},{13,... | collective-permute-start | bytes 6291464 | tf_op jit(solution)/shard_map/ppermute | solution.py:505
  99.1 12.6 %copy-start = (f32[16]{0:T(128)}, f32[16]{0:T(128)S(1)}, u32[]{:S(2)}) copy-start(f32[16]{0:T(128)S(1)} %slice_reduce_fusion) | copy-start | bytes 196

commit v3 on v2

--- a/solution.py
+++ b/solution.py
@@ -21,12 +21,12 @@
 COLS = 1024
 HEADS = 8
 OWN, FAR, NEAR, LAST = 0, 1, 2, 3
-TABLE_OF = (0, 0, 1, 0)
+TABLE_OF = (0, 1, 2, 0)
 F32, BF16 = jnp.float32, jnp.bfloat16
 
 
 def attend_kernel(hid, pos, freq, w_q, w_k, w_v, w_o, out, peak,
-                  hbuf, wq, wk, wv, wo, qbuf, kbuf, vbuf, acc, run_max, run_sum, o_all, cos_t, sin_t, pos_all,
+                  hbuf, wk, wv, w_pair, qbuf, kbuf, vbuf, acc, run_max, run_sum, cos_t, sin_t, pos_all,
                   bias, top_all, wsem, send, recv, psend, precv, osem, tsend, trecv):
     x = lax.axis_index("cp")
     d = lax.axis_index("dp")
@@ -47,9 +47,9 @@
                                             device_id={"dp": dp, "cp": cp}, device_id_type=MESH)
 
     w_copies = [pltpu.make_async_copy(src.at[:, pl.ds(col0, COLS)], dst, wsem.at[i])
-                for i, (src, dst) in enumerate(((w_k, wk), (w_v, wv), (w_q, wq)))]
-    w_copies.append(pltpu.make_async_copy(w_o.at[:, pl.ds(COLS, COLS)], wo, wsem.at[3]))
-    wo_low = pltpu.make_async_copy(w_o.at[:, pl.ds(0, COLS)], wq, wsem.at[6])
+                for i, (src, dst) in enumerate(((w_k, wk), (w_v, wv), (w_q, w_pair.at[0])))]
+    w_copies.append(pltpu.make_async_copy(w_o.at[:, pl.ds(COLS, COLS)], w_pair.at[1], wsem.at[3]))
+    wo_low = pltpu.make_async_copy(w_o.at[:, pl.ds(0, COLS)], w_pair.at[0], wsem.at[6])
 
     def half_rows(j):
         return pl.ds(pl.multiple_of(j * HALF, HALF), HALF)
@@ -110,7 +110,7 @@
         col_i = lax.broadcasted_iota(jnp.int32, (64, 128), 1)
         low = col_i < 64
 
-        def block(b, carry):
+        def one(b):
             if kind == OWN:
                 line = pos[pl.ds(b, 1), :]
             else:
@@ -126,9 +126,13 @@
             cos_t[pl.ds(at + 64, 64), :] = jnp.where(low, cos_r, cos_a)
             sin_t[pl.ds(at, 64), :] = jnp.where(low, -sin_a, sin_r)
             sin_t[pl.ds(at + 64, 64), :] = jnp.where(low, -sin_r, sin_a)
+
+        def block(b, carry):
+            one(2 * b)
+            one(2 * b + 1)
             return carry
 
-        lax.fori_loop(0, 4, block, 0)
+        lax.fori_loop(0, 2, block, 0)
 
     def rotate(t, cos_v, sin_v):
         parts = []
@@ -146,7 +150,7 @@
         vbuf[at, :] = jnp.dot(h, wv[...], preferred_element_type=F32).astype(BF16)
         if with_q:
             q_at = pl.ds(pl.multiple_of(half * HALF, HALF), HALF)
-            qbuf[kind, q_at, :] = rotate(jnp.dot(h, wq[...], preferred_element_type=F32), cos_v, sin_v)
+            qbuf[kind, q_at, :] = rotate(jnp.dot(h, w_pair[0], preferred_element_type=F32), cos_v, sin_v)
 
     def tile(slot, piece, diagonal):
         key0 = pl.multiple_of(piece * PIECE, PIECE)
@@ -212,6 +216,10 @@
     bias[...] = jnp.where(lax.broadcasted_iota(jnp.int32, (HALF, HALF), 0) >= lax.broadcasted_iota(jnp.int32, (HALF, HALF), 1),
                           0.0, -jnp.inf)
     tables(OWN)
+    for copy in pos_copies:
+        copy.wait_recv()
+    tables(FAR)
+    tables(NEAR)
     for i in range(3):
         w_copies[i].wait()
 
@@ -221,18 +229,18 @@
         return carry
 
     lax.fori_loop(0, 2, own_half, 0)
-    for copy in pos_copies:
-        copy.wait_recv()
-    tables(FAR)
-    tables(NEAR)
 
     def far_half(j, carry):
         arrive(FAR, j)
+
+        @pl.when(x != 2)
+        def _():
+            arrive(NEAR, j)
+
         project(FAR, j, True)
 
         @pl.when(x != 2)
         def _():
-            arrive(NEAR, j)
             project(NEAR, j, False)
         return carry
 
@@ -259,51 +267,26 @@
 
     lax.fori_loop(0, 3, near_tile, 0)
 
-    exchange = remote(qbuf.at[jnp.where(home, FAR, OWN)], o_all.at[core], osem.at[0], osem.at[1], partner, x)
-
+    early = 1 - later
+    mine = jnp.where(core == 0, early, later)
+    exchange = remote(qbuf.at[1 - mine], qbuf.at[2], osem.at[0], osem.at[1], partner, x)
     own_rows = pl.ds(pl.multiple_of(x * PIECE, PIECE), PIECE)
 
     def out_copy(part):
-        cols = pl.ds(part * COLS, COLS)
+        cols = pl.ds(pl.multiple_of(part * COLS, COLS), COLS)
         return pltpu.make_async_copy(hbuf.at[own_rows, cols], out.at[:, cols], wsem.at[7 + part])
 
-    def section(slot):
-        mine = (home & (slot == OWN)) | (away & (slot == FAR))
-
-        def head(h, carry):
-            cols = pl.ds(pl.multiple_of(h * HEAD_DIM, HEAD_DIM), HEAD_DIM)
+    def finish(slot):
+        for h in range(HEADS):
+            cols = pl.ds(h * HEAD_DIM, HEAD_DIM)
             total = jnp.sum(run_sum[slot, h, :, :], axis=1, keepdims=True)
-            value = (acc[slot, :, cols] / total).astype(BF16)
-
-            @pl.when(mine)
-            def _():
-                o_all[core, :, cols] = value
-
-            @pl.when(jnp.logical_not(mine))
-            def _():
-                qbuf[slot, :, cols] = value
-            return carry
-
-        lax.fori_loop(0, HEADS, head, 0)
-
-        @pl.when(jnp.logical_not(mine))
-        def _():
-            exchange.start()
-
-        @pl.when(mine)
-        def _():
-            exchange.wait_recv()
-
-            for part, w in enumerate((wq, wo)):
-                def out_block(n, carry):
-                    cols = pl.ds(pl.multiple_of(n * 512, 512), 512)
-                    value = (jnp.dot(o_all[0], w[:COLS, cols], preferred_element_type=F32)
-                             + jnp.dot(o_all[1], w[COLS:, cols], preferred_element_type=F32))
-                    hbuf[own_rows, pl.ds(pl.multiple_of(part * COLS + n * 512, 512), 512)] = value.astype(BF16)
-                    return carry
-
-                lax.fori_loop(0, COLS // 512, out_block, 0)
-                out_copy(part).start()
+            qbuf[slot, :, cols] = (acc[slot, :, cols] / total).astype(BF16)
+
+    def output(part):
+        heads = jnp.concatenate([qbuf[jnp.where(core == 0, mine, 2)], qbuf[jnp.where(core == 0, 2, mine)]], axis=1)
+        value = jnp.dot(heads, w_pair[part], preferred_element_type=F32)
+        hbuf[own_rows, pl.ds(pl.multiple_of(part * COLS, COLS), COLS)] = value.astype(BF16)
+        out_copy(part).start()
 
     w_copies[3].wait()
     wo_low.wait()
@@ -311,7 +294,21 @@
 
     @pl.when(outer)
     def _():
-        section(1 - later)
+        finish(early)
+
+        @pl.when(core == 1)
+        def _():
+            exchange.start()
+
+        @pl.when(core == 0)
+        def _():
+            exchange.wait_recv()
+
+            def one(part, carry):
+                output(part)
+                return carry
+
+            lax.fori_loop(0, 2, one, 0)
 
     @pl.when(x != 1)
     def _():
@@ -329,32 +326,51 @@
 
     lax.fori_loop(0, 2, last_tile, 0)
 
+    finish(later)
+
+    @pl.when(core == 0)
+    def _():
+        exchange.start()
+
     top_all[0] = jnp.full((2 * HEADS, 128), -jnp.inf, F32)
-
-    def head_top(h, carry):
+    for h in range(HEADS):
         top = jnp.maximum(jnp.max(run_max[0, h, :, :], axis=0, keepdims=True), jnp.max(run_max[1, h, :, :], axis=0, keepdims=True))
         top_all[0, pl.ds(core * HEADS + h, 1), :] = top * SCALE
-        return carry
-
-    lax.fori_loop(0, HEADS, head_top, 0)
     top_copies = [remote(top_all.at[0], top_all.at[k], tsend.at[k - 1], trecv.at[k - 1], d, lax.rem(x + k, 4)) for k in range(1, 4)]
-    for copy in top_copies:
+    top_copies.append(remote(top_all.at[4], top_all.at[5], tsend.at[3], trecv.at[3], partner, x))
+    for copy in top_copies[:3]:
         copy.start()
 
-    def end_section(i, carry):
-        section(jnp.where(i == 0, 1 - later, later))
-        return carry
-
-    lax.fori_loop(jnp.where(outer, 1, 0), 2, end_section, 0)
+    @pl.when(jnp.logical_not(outer))
+    def _():
+        finish(early)
+
+        @pl.when(core == 1)
+        def _():
+            exchange.start()
+
+    busy = (core == 1) | jnp.logical_not(outer)
+
+    @pl.when(busy)
+    def _():
+        exchange.wait_recv()
+        output(0)
 
     best = top_all[0]
-    for k, copy in enumerate(top_copies):
-        copy.wait_recv()
+    for k in range(3):
+        top_copies[k].wait_recv()
         best = jnp.maximum(best, top_all[k + 1])
-    peak[...] = best
+    top_all[4] = best
+    top_copies[3].start()
+
+    @pl.when(busy)
+    def _():
+        output(1)
+
+    top_copies[3].wait_recv()
+    peak[...] = jnp.maximum(top_all[4], top_all[5])
     for copy in top_copies:
         copy.wait_send()
-
     for part in range(2):
         out_copy(part).wait()
 
@@ -405,16 +421,14 @@
         out_specs=[any_spec, vmem],
         scratch_shapes=[
             pltpu.VMEM((4 * PIECE, MODEL), BF16),
-            pltpu.VMEM((MODEL, COLS), BF16), pltpu.VMEM((MODEL, COLS), BF16), pltpu.VMEM((MODEL, COLS), BF16),
-            pltpu.VMEM((MODEL, COLS), BF16),
-            pltpu.VMEM((2, PIECE, COLS), BF16), pltpu.VMEM((4 * PIECE, COLS), BF16), pltpu.VMEM((4 * PIECE, COLS), BF16),
+            pltpu.VMEM((MODEL, COLS), BF16), pltpu.VMEM((MODEL, COLS), BF16), pltpu.VMEM((2, MODEL, COLS), BF16),
+            pltpu.VMEM((3, PIECE, COLS), BF16), pltpu.VMEM((4 * PIECE, COLS), BF16), pltpu.VMEM((4 * PIECE, COLS), BF16),
             pltpu.VMEM((2, PIECE, COLS), F32), pltpu.VMEM((2, HEADS, PIECE, 128), F32), pltpu.VMEM((2, HEADS, PIECE, 128), F32),
-            pltpu.VMEM((2, PIECE, COLS), BF16),
-            pltpu.VMEM((2 * PIECE, 128), F32), pltpu.VMEM((2 * PIECE, 128), F32), pltpu.VMEM((4, 4, 128), jnp.int32),
-            pltpu.VMEM((HALF, HALF), F32), pltpu.VMEM((4, 2 * HEADS, 128), F32),
+            pltpu.VMEM((3 * PIECE, 128), F32), pltpu.VMEM((3 * PIECE, 128), F32), pltpu.VMEM((4, 4, 128), jnp.int32),
+            pltpu.VMEM((HALF, HALF), F32), pltpu.VMEM((6, 2 * HEADS, 128), F32),
             pltpu.SemaphoreType.DMA((9,)), pltpu.SemaphoreType.DMA((14,)), pltpu.SemaphoreType.DMA((8,)),
             pltpu.SemaphoreType.DMA((3,)), pltpu.SemaphoreType.DMA((3,)), pltpu.SemaphoreType.DMA((2,)),
-            pltpu.SemaphoreType.DMA((3,)), pltpu.SemaphoreType.DMA((3,)),
+            pltpu.SemaphoreType.DMA((4,)), pltpu.SemaphoreType.DMA((4,)),
         ],
         compiler_params=pltpu.CompilerParams(collective_id=0, has_side_effects=True, vmem_limit_bytes=67043328),
         cost_estimate=pl.CostEstimate(flops=31_000_000_000, bytes_accessed=26_000_000, transcendentals=11_000_000),
@@ -427,7 +441,6 @@
     d = lax.axis_index("dp")
     core, y, z = lax.rem(d, 2), lax.rem(d // 2, n_y), d // (2 * n_y)
     rounds = [
-        [(d + 1 - 2 * core, x)],
         [((z * n_y + lax.rem(y + k, n_y)) * 2 + core, x) for k in range(1, n_y)],
         [((lax.rem(z + k, n_z) * n_y + y) * 2 + core, x) for k in range(1, n_z)],
     ]
@@ -464,7 +477,7 @@
 
 
 def global_peak(peak, sizes):
-    n_copies = 1 + sum(n - 1 for n in sizes)
+    n_copies = sum(n - 1 for n in sizes)
     vmem = pl.BlockSpec(memory_space=pltpu.VMEM)
     shape = peak.shape
     return pl.pallas_call(
@@ -472,7 +485,7 @@
         name="global_peak",
         out_shape=jax.ShapeDtypeStruct(shape, F32),
         in_specs=[vmem], out_specs=vmem,
-        scratch_shapes=[pltpu.VMEM((3,) + shape, F32), pltpu.VMEM((n_copies,) + shape, F32),
+        scratch_shapes=[pltpu.VMEM((2,) + shape, F32), pltpu.VMEM((n_copies,) + shape, F32),
                         pltpu.SemaphoreType.DMA((n_copies,)), pltpu.SemaphoreType.DMA((n_copies,))],
         compiler_params=pltpu.CompilerParams(collective_id=1, has_side_effects=True),
         cost_estimate=pl.CostEstimate(flops=10_000_000, bytes_accessed=8192, transcendentals=0),

time: 113 us -> 112 us (level)
  starting transfers between devices: 10 us -> 5.97 us
  Pallas kernels: 87.6 us -> 90.4 us
    ppermute x1, starting transfers between devices: 10 us -> 5.97 us  [device_body(): swapped = lax.ppermute(out, ('dp', 'cp'), swap)]
    pallas_call x1, Pallas kernels: 70.7 us -> 73.7 us  [attend(): pl.pallas_call(attend_kernel, name='attend', out_shape=[jax.ShapeDtypeStr...]
where the time goes in v3:
time: 112 us
  Pallas kernels  90.4 us (81%)
  other arithmetic  12.5 us (11%)
  starting transfers between devices  5.97 us (5%)
  local copies, waits for them, and re-layouts  2.21 us (2%)
    pallas_call x1, Pallas kernels, attend(): pl.pallas_call(attend_kernel, name='attend', out_shape=[jax.ShapeDtypeStr...  73.7 us
    pallas_call x1, Pallas kernels, global_peak(): pl.pallas_call(functools.partial(peak_kernel, sizes), name='global_peak',...  16.8 us
    convert_element_type x1, other arithmetic, clip_weights(): (w_k.astype(F32) * col_factor).astype(BF16)  12.5 us
    ppermute x1, starting transfers between devices, device_body(): swapped = lax.ppermute(out, ('dp', 'cp'), swap)  5.97 us
  transfers between devices with their start and end apart: 1, of which 0 were waited for; matrix products, arithmetic and copies ran while one was open for 12% of the time, Pallas kernels for 15%

profile of v3, /device:TPU:6, one launch (start us, length us, event | category | flops | bytes accessed | tf_op | source)
XLA Modules:
  0.0 111.8 jit_solution(17031806317188905837)
XLA Ops:
  0.6 73.7 %attend.1 = (bf16[512,2048]{1,0:T(8,128)(2,1)}, f32[16,128]{1,0:T(8,128)}) custom-call(bf16[512,2048]{1,0:T(8,128)(2,1)} %bitcast.6, s32[4,128]{1,0:T(4,128)} %bitcast.7, f32[1,128]{1,0:T(1,128)} %constant.6.clone.freq, bf16[2048,2048]{1,0:T(8,128)(2,1)} %w_q.1, bf16[2048,2048]{1,0:T(8,128)(2,1)} %w_k.1, bf16[2048,2048]{1,0:T(8,128)(2,1)} %w_v.1, ...), custom_call_target="tpu_custom_call" | custom-call | flops 31000000512 | bytes 26000000 | tf_op jit(solution)/shard_map/attend/pallas_call | solution.py:416
  74.3 6.0 %collective-permute-start = (bf16[512,2048]{1,0:T(8,128)(2,1)}, bf16[512,2048]{1,0:T(8,128)(2,1)S(1)}, u32[]{:S(2)}, u32[]{:S(2)}) collective-permute-start(bf16[512,2048]{1,0:T(8,128)(2,1)} %get-tuple-element.6), channel_id=1, source_target_pairs={{4,3},{0,0},{5,2},{1,1},{2,5},{6,6},{3,4},{7,7},{12,11},{8,8},{13,... | collective-permute-start | bytes 6291464 | tf_op jit(solution)/shard_map/ppermute | solution.py:518
  80.3 16.8 %global_peak.1 = f32[16,128]{1,0:T(8,128)} custom-call(f32[16,128]{1,0:T(8,128)} %get-tuple-element.7.peak), custom_call_target="tpu_custom_call" | custom-call | flops 10000000 | bytes 8192 | tf_op jit(solution)/shard_map/global_peak/pallas_call | solution.py:483
  97.1 0.8 slice_reduce_fusion
  97.9 0.0 copy-start
  97.9 0.1 broadcast_bitcast_fusion
  98.0 12.5 %multiply_convert_fusion = (bf16[2048,2048]{1,0:T(8,128)(2,1)}, bf16[2048,2048]{1,0:T(8,128)(2,1)}) fusion(bf16[2048,2048]{1,0:T(8,128)(2,1)} %w_k.1, f32[2048]{0:T(1024)S(1)} %broadcast_bitcast_fusion, bf16[2048,2048]{1,0:T(8,128)(2,1)} %w_q.1), kind=kLoop, calls=%fused_computation | loop fusion | flops 25165824 | bytes 33562624 | tf_op jit(solution)/shard_map/convert_element_type | solution.py:498
  110.5 0.0 copy-done
  110.5 0.0 collective-permute-done
  110.5 1.3 %copy.12 = bf16[1,512,2048]{2,1,0:T(8,128)(2,1)} copy(bf16[1,512,2048]{2,1,0:T(8,128)(2,1)S(1)} %bitcast.5) | data formatting | bytes 4194304
  (1 shorter events, 0.0 us)
Async XLA Ops:
  74.3 36.2 %collective-permute-start = (bf16[512,2048]{1,0:T(8,128)(2,1)}, bf16[512,2048]{1,0:T(8,128)(2,1)S(1)}, u32[]{:S(2)}, u32[]{:S(2)}) collective-permute-start(bf16[512,2048]{1,0:T(8,128)(2,1)} %get-tuple-element.6), channel_id=1, source_target_pairs={{4,3},{0,0},{5,2},{1,1},{2,5},{6,6},{3,4},{7,7},{12,11},{8,8},{13,... | collective-permute-start | bytes 6291464 | tf_op jit(solution)/shard_map/ppermute | solution.py:518
  97.9 12.6 %copy-start = (f32[16]{0:T(128)}, f32[16]{0:T(128)S(1)}, u32[]{:S(2)}) copy-start(f32[16]{0:T(128)S(1)} %slice_reduce_fusion) | copy-start | bytes 196

commit v4 on v3

--- a/solution.py
+++ b/solution.py
@@ -229,6 +229,10 @@
         return carry
 
     lax.fori_loop(0, 2, own_half, 0)
+    @pl.when(x >= 0)
+    def _():
+        tile(OWN, x, True)
+
 
     def far_half(j, carry):
         arrive(FAR, j)
@@ -248,11 +252,9 @@
     wo_low.start()
     tables(LAST)
 
-    def diagonal_tile(slot, carry):
-        tile(slot, jnp.where(slot == OWN, x, far_x), True)
-        return carry
-
-    lax.fori_loop(0, 2, diagonal_tile, 0)
+    @pl.when(x >= 0)
+    def _():
+        tile(FAR, far_x, True)
 
     later = jnp.where(x < 2, FAR, OWN)
 
@@ -288,8 +290,6 @@
         hbuf[own_rows, pl.ds(pl.multiple_of(part * COLS, COLS), COLS)] = value.astype(BF16)
         out_copy(part).start()
 
-    w_copies[3].wait()
-    wo_low.wait()
     outer = (x == 0) | (x == 3)
 
     @pl.when(outer)
@@ -299,16 +299,6 @@
         @pl.when(core == 1)
         def _():
             exchange.start()
-
-        @pl.when(core == 0)
-        def _():
-            exchange.wait_recv()
-
-            def one(part, carry):
-                output(part)
-                return carry
-
-            lax.fori_loop(0, 2, one, 0)
 
     @pl.when(x != 1)
     def _():
@@ -349,11 +339,12 @@
         def _():
             exchange.start()
 
-    busy = (core == 1) | jnp.logical_not(outer)
-
-    @pl.when(busy)
-    def _():
-        exchange.wait_recv()
+    w_copies[3].wait()
+    wo_low.wait()
+    exchange.wait_recv()
+
+    @pl.when(x >= 0)
+    def _():
         output(0)
 
     best = top_all[0]
@@ -363,7 +354,7 @@
     top_all[4] = best
     top_copies[3].start()
 
-    @pl.when(busy)
+    @pl.when(x >= 0)
     def _():
         output(1)
 
@@ -492,10 +483,25 @@
     )(peak)
 
 
-def clip_weights(head_max, w_q, w_k):
-    factor = jnp.where(head_max > TAU_CLIP, jnp.sqrt(TAU_CLIP / head_max), 1.0)
-    col_factor = jnp.repeat(factor, HEAD_DIM)[None, :]
-    return (w_q.astype(F32) * col_factor).astype(BF16), (w_k.astype(F32) * col_factor).astype(BF16)
+def clip_kernel(best, w_q, w_k, q_new, k_new):
+    factor = jnp.where(best[...] > TAU_CLIP, jnp.sqrt(TAU_CLIP / best[...]), 1.0)
+    for h in range(2 * HEADS):
+        cols = pl.ds(h * HEAD_DIM, HEAD_DIM)
+        q_new[:, cols] = (w_q[:, cols].astype(F32) * factor[h:h + 1, :]).astype(BF16)
+        k_new[:, cols] = (w_k[:, cols].astype(F32) * factor[h:h + 1, :]).astype(BF16)
+
+
+def clip_weights(best, w_q, w_k):
+    block = pl.BlockSpec((256, MODEL), lambda i: (i, 0))
+    return pl.pallas_call(
+        clip_kernel,
+        name="clip",
+        grid=(MODEL // 256,),
+        out_shape=[jax.ShapeDtypeStruct(w_q.shape, BF16)] * 2,
+        in_specs=[pl.BlockSpec(best.shape, lambda i: (0, 0)), block, block],
+        out_specs=[block, block],
+        cost_estimate=pl.CostEstimate(flops=1_000_000_000, bytes_accessed=4 * MODEL * MODEL * 2, transcendentals=0),
+    )(best, w_q, w_k)
 
 
 def solution(mesh):
@@ -516,9 +522,9 @@
         freq = jnp.asarray(np.concatenate([inv_freq, inv_freq])[None, :], F32)
         out, peak = attend(hidden[0], pos_ids.reshape(4, 128), freq, w_q, w_k, w_v, w_o)
         swapped = lax.ppermute(out, ("dp", "cp"), swap)
-        head_max = global_peak(peak, sizes)[:, 0]
-        w_q_new, w_k_new = clip_weights(head_max, w_q, w_k)
-        return swapped[None], head_max, w_q_new, w_k_new
+        best = global_peak(peak, sizes)
+        w_q_new, w_k_new = clip_weights(best, w_q, w_k)
+        return swapped[None], best[:, 0], w_q_new, w_k_new
 
     return jax.shard_map(
         device_body,

time: 112 us -> 105 us (0.938)
  other arithmetic: 12.5 us -> 0 us
  Pallas kernels: 90.4 us -> 97.5 us
    pallas_call x0 -> x1, Pallas kernels: none -> 16.2 us  [clip_weights(): pl.pallas_call(clip_kernel, name='clip', grid=(MODEL // 256,), out_shape=...]
    convert_element_type x1 -> x0, other arithmetic: 12.5 us -> none  [clip_weights(): (w_k.astype(F32) * col_factor).astype(BF16)]
    pallas_call x1, Pallas kernels: 73.7 us -> 63.8 us  [attend(): pl.pallas_call(attend_kernel, name='attend', out_shape=[jax.ShapeDtypeStr...]
  transfers between devices with their start and end apart: 1 -> 1, of which waited for: 0 -> 0; matrix products, arithmetic and copies ran while one was open for 12% -> 1% of each run, Pallas kernels for 15% -> 32%
where the time goes in v4:
time: 105 us
  Pallas kernels  97.5 us (93%)
  starting transfers between devices  4.88 us (5%)
  local copies, waits for them, and re-layouts  1.95 us (2%)
    pallas_call x1, Pallas kernels, attend(): pl.pallas_call(attend_kernel, name='attend', out_shape=[jax.ShapeDtypeStr...  63.8 us
    pallas_call x1, Pallas kernels, global_peak(): pl.pallas_call(functools.partial(peak_kernel, sizes), name='global_peak',...  17.5 us
    pallas_call x1, Pallas kernels, clip_weights(): pl.pallas_call(clip_kernel, name='clip', grid=(MODEL // 256,), out_shape=...  16.2 us
    ppermute x1, starting transfers between devices, device_body(): swapped = lax.ppermute(out, ('dp', 'cp'), swap)  4.88 us
  transfers between devices with their start and end apart: 1, of which 0 were waited for; matrix products, arithmetic and copies ran while one was open for 1% of the time, Pallas kernels for 32%

profile of v4, /device:TPU:6, one launch (start us, length us, event | category | flops | bytes accessed | tf_op | source)
XLA Modules:
  0.0 105.0 jit_solution(5107060532791574882)
XLA Ops:
  0.6 63.8 %attend.1 = (bf16[512,2048]{1,0:T(8,128)(2,1)}, f32[16,128]{1,0:T(8,128)}) custom-call(bf16[512,2048]{1,0:T(8,128)(2,1)} %bitcast.4, s32[4,128]{1,0:T(4,128)} %bitcast.5, f32[1,128]{1,0:T(1,128)} %constant.2.clone.freq, bf16[2048,2048]{1,0:T(8,128)(2,1)} %w_q.3, bf16[2048,2048]{1,0:T(8,128)(2,1)} %w_k.3, bf16[2048,2048]{1,0:T(8,128)(2,1)} %w_v.1, ...), custom_call_target="tpu_custom_call" | custom-call | flops 31000000512 | bytes 26000000 | tf_op jit(solution)/shard_map/attend/pallas_call | solution.py:407
  64.5 4.9 %collective-permute-start = (bf16[512,2048]{1,0:T(8,128)(2,1)}, bf16[512,2048]{1,0:T(8,128)(2,1)S(1)}, u32[]{:S(2)}, u32[]{:S(2)}) collective-permute-start(bf16[512,2048]{1,0:T(8,128)(2,1)} %get-tuple-element.8), channel_id=1, source_target_pairs={{4,3},{0,0},{5,2},{1,1},{2,5},{6,6},{3,4},{7,7},{12,11},{8,8},{13,... | collective-permute-start | bytes 6291464 | tf_op jit(solution)/shard_map/ppermute | solution.py:524
  69.4 17.5 %global_peak.1.best = f32[16,128]{1,0:T(8,128)} custom-call(f32[16,128]{1,0:T(8,128)} %get-tuple-element.9.peak), custom_call_target="tpu_custom_call" | custom-call | flops 10000000 | bytes 8192 | tf_op jit(solution)/shard_map/global_peak/pallas_call | solution.py:474
  86.8 0.0 copy-start
  86.8 16.2 %clip.1 = (bf16[2048,2048]{1,0:T(8,128)(2,1)}, bf16[2048,2048]{1,0:T(8,128)(2,1)}) custom-call(f32[16,128]{1,0:T(8,128)} %global_peak.1.best, bf16[2048,2048]{1,0:T(8,128)(2,1)} %w_q.3, bf16[2048,2048]{1,0:T(8,128)(2,1)} %w_k.3), custom_call_target="tpu_custom_call" | custom-call | flops 1000000000 | bytes 33554432 | tf_op jit(solution)/shard_map/clip/pallas_call | solution.py:496
  103.0 0.0 copy-done
  103.0 0.6 slice_reduce_fusion
  103.7 0.0 collective-permute-done
  103.7 1.3 %copy.12 = bf16[1,512,2048]{2,1,0:T(8,128)(2,1)} copy(bf16[1,512,2048]{2,1,0:T(8,128)(2,1)S(1)} %bitcast.3) | data formatting | bytes 4194304
Async XLA Ops:
  64.5 39.2 %collective-permute-start = (bf16[512,2048]{1,0:T(8,128)(2,1)}, bf16[512,2048]{1,0:T(8,128)(2,1)S(1)}, u32[]{:S(2)}, u32[]{:S(2)}) collective-permute-start(bf16[512,2048]{1,0:T(8,128)(2,1)} %get-tuple-element.8), channel_id=1, source_target_pairs={{4,3},{0,0},{5,2},{1,1},{2,5},{6,6},{3,4},{7,7},{12,11},{8,8},{13,... | collective-permute-start | bytes 6291464 | tf_op jit(solution)/shard_map/ppermute | solution.py:524
  86.8 16.2 %copy-start = (f32[16,128]{1,0:T(8,128)S(1)}, f32[16,128]{1,0:T(8,128)}, u32[]{:S(2)}) copy-start(f32[16,128]{1,0:T(8,128)} %global_peak.1.best) | copy-start | bytes 24580

commit v5 on v4

--- a/solution.py
+++ b/solution.py
@@ -483,25 +483,10 @@
     )(peak)
 
 
-def clip_kernel(best, w_q, w_k, q_new, k_new):
-    factor = jnp.where(best[...] > TAU_CLIP, jnp.sqrt(TAU_CLIP / best[...]), 1.0)
-    for h in range(2 * HEADS):
-        cols = pl.ds(h * HEAD_DIM, HEAD_DIM)
-        q_new[:, cols] = (w_q[:, cols].astype(F32) * factor[h:h + 1, :]).astype(BF16)
-        k_new[:, cols] = (w_k[:, cols].astype(F32) * factor[h:h + 1, :]).astype(BF16)
-
-
-def clip_weights(best, w_q, w_k):
-    block = pl.BlockSpec((256, MODEL), lambda i: (i, 0))
-    return pl.pallas_call(
-        clip_kernel,
-        name="clip",
-        grid=(MODEL // 256,),
-        out_shape=[jax.ShapeDtypeStruct(w_q.shape, BF16)] * 2,
-        in_specs=[pl.BlockSpec(best.shape, lambda i: (0, 0)), block, block],
-        out_specs=[block, block],
-        cost_estimate=pl.CostEstimate(flops=1_000_000_000, bytes_accessed=4 * MODEL * MODEL * 2, transcendentals=0),
-    )(best, w_q, w_k)
+def clip_weights(head_max, w_q, w_k):
+    factor = jnp.where(head_max > TAU_CLIP, jnp.sqrt(TAU_CLIP / head_max), 1.0)
+    col_factor = jnp.repeat(factor, HEAD_DIM)[None, :]
+    return (w_q.astype(F32) * col_factor).astype(BF16), (w_k.astype(F32) * col_factor).astype(BF16)
 
 
 def solution(mesh):
@@ -522,9 +507,9 @@
         freq = jnp.asarray(np.concatenate([inv_freq, inv_freq])[None, :], F32)
         out, peak = attend(hidden[0], pos_ids.reshape(4, 128), freq, w_q, w_k, w_v, w_o)
         swapped = lax.ppermute(out, ("dp", "cp"), swap)
-        best = global_peak(peak, sizes)
-        w_q_new, w_k_new = clip_weights(best, w_q, w_k)
-        return swapped[None], best[:, 0], w_q_new, w_k_new
+        head_max = global_peak(peak, sizes)[:, 0]
+        w_q_new, w_k_new = clip_weights(head_max, w_q, w_k)
+        return swapped[None], head_max, w_q_new, w_k_new
 
     return jax.shard_map(
         device_body,

time: 105 us -> 102 us (0.971)
  Pallas kernels: 97.5 us -> 81.3 us
  other arithmetic: 0 us -> 12.5 us
    pallas_call x1 -> x0, Pallas kernels: 16.2 us -> none  [clip_weights(): pl.pallas_call(clip_kernel, name='clip', grid=(MODEL // 256,), out_shape=...]
    convert_element_type x0 -> x1, other arithmetic: none -> 12.5 us  [clip_weights(): (w_k.astype(F32) * col_factor).astype(BF16)]
  transfers between devices with their start and end apart: 1 -> 1, of which waited for: 0 -> 0; matrix products, arithmetic and copies ran while one was open for 1% -> 13% of each run, Pallas kernels for 32% -> 17%
where the time goes in v5:
time: 102 us
  Pallas kernels  81.3 us (80%)
  other arithmetic  12.5 us (12%)
  starting transfers between devices  4.88 us (5%)
  local copies, waits for them, and re-layouts  2.21 us (2%)
    pallas_call x1, Pallas kernels, attend(): pl.pallas_call(attend_kernel, name='attend', out_shape=[jax.ShapeDtypeStr...  63.8 us
    pallas_call x1, Pallas kernels, global_peak(): pl.pallas_call(functools.partial(peak_kernel, sizes), name='global_peak',...  17.5 us
    convert_element_type x1, other arithmetic, clip_weights(): (w_k.astype(F32) * col_factor).astype(BF16)  12.5 us
    ppermute x1, starting transfers between devices, device_body(): swapped = lax.ppermute(out, ('dp', 'cp'), swap)  4.88 us
  transfers between devices with their start and end apart: 1, of which 0 were waited for; matrix products, arithmetic and copies ran while one was open for 13% of the time, Pallas kernels for 17%

profile of v5, /device:TPU:6, one launch (start us, length us, event | category | flops | bytes accessed | tf_op | source)
XLA Modules:
  0.0 101.6 jit_solution(13808943266290825121)
XLA Ops:
  0.6 63.8 %attend.1 = (bf16[512,2048]{1,0:T(8,128)(2,1)}, f32[16,128]{1,0:T(8,128)}) custom-call(bf16[512,2048]{1,0:T(8,128)(2,1)} %bitcast.6, s32[4,128]{1,0:T(4,128)} %bitcast.7, f32[1,128]{1,0:T(1,128)} %constant.6.clone.freq, bf16[2048,2048]{1,0:T(8,128)(2,1)} %w_q.1, bf16[2048,2048]{1,0:T(8,128)(2,1)} %w_k.1, bf16[2048,2048]{1,0:T(8,128)(2,1)} %w_v.1, ...), custom_call_target="tpu_custom_call" | custom-call | flops 31000000512 | bytes 26000000 | tf_op jit(solution)/shard_map/attend/pallas_call | solution.py:407
  64.5 4.9 %collective-permute-start = (bf16[512,2048]{1,0:T(8,128)(2,1)}, bf16[512,2048]{1,0:T(8,128)(2,1)S(1)}, u32[]{:S(2)}, u32[]{:S(2)}) collective-permute-start(bf16[512,2048]{1,0:T(8,128)(2,1)} %get-tuple-element.6), channel_id=1, source_target_pairs={{4,3},{0,0},{5,2},{1,1},{2,5},{6,6},{3,4},{7,7},{12,11},{8,8},{13,... | collective-permute-start | bytes 6291464 | tf_op jit(solution)/shard_map/ppermute | solution.py:509
  69.4 17.5 %global_peak.1 = f32[16,128]{1,0:T(8,128)} custom-call(f32[16,128]{1,0:T(8,128)} %get-tuple-element.7.peak), custom_call_target="tpu_custom_call" | custom-call | flops 10000000 | bytes 8192 | tf_op jit(solution)/shard_map/global_peak/pallas_call | solution.py:474
  86.8 0.8 slice_reduce_fusion
  87.6 0.0 copy-start
  87.7 0.1 broadcast_bitcast_fusion
  87.7 12.5 %multiply_convert_fusion = (bf16[2048,2048]{1,0:T(8,128)(2,1)}, bf16[2048,2048]{1,0:T(8,128)(2,1)}) fusion(bf16[2048,2048]{1,0:T(8,128)(2,1)} %w_k.1, f32[2048]{0:T(1024)S(1)} %broadcast_bitcast_fusion, bf16[2048,2048]{1,0:T(8,128)(2,1)} %w_q.1), kind=kLoop, calls=%fused_computation | loop fusion | flops 25165824 | bytes 33562624 | tf_op jit(solution)/shard_map/convert_element_type | solution.py:489
  100.2 0.0 copy-done
  100.2 0.0 collective-permute-done
  100.2 1.3 %copy.12 = bf16[1,512,2048]{2,1,0:T(8,128)(2,1)} copy(bf16[1,512,2048]{2,1,0:T(8,128)(2,1)S(1)} %bitcast.5) | data formatting | bytes 4194304
  (1 shorter events, 0.0 us)
Async XLA Ops:
  64.5 35.8 %collective-permute-start = (bf16[512,2048]{1,0:T(8,128)(2,1)}, bf16[512,2048]{1,0:T(8,128)(2,1)S(1)}, u32[]{:S(2)}, u32[]{:S(2)}) collective-permute-start(bf16[512,2048]{1,0:T(8,128)(2,1)} %get-tuple-element.6), channel_id=1, source_target_pairs={{4,3},{0,0},{5,2},{1,1},{2,5},{6,6},{3,4},{7,7},{12,11},{8,8},{13,... | collective-permute-start | bytes 6291464 | tf_op jit(solution)/shard_map/ppermute | solution.py:509
  87.6 12.6 %copy-start = (f32[16]{0:T(128)}, f32[16]{0:T(128)S(1)}, u32[]{:S(2)}) copy-start(f32[16]{0:T(128)S(1)} %slice_reduce_fusion) | copy-start | bytes 196
